TPU v7x, 32 devices: a whole 2x2x4 slice. The times are simulated.
32 devices in a mesh: front: 8 (over y, x, core), sub: 4 (over z).
Axes of the slice: x: 2, y: 2, z: 4, core: 2. Of those that a mesh axis runs over, the one named last changes fastest.
Arguments:
- row_values: float32 [4096, 1024], P(('front', 'sub')), may hold values from -0.12 to 0.12
- front_of_row: int32 [4096, 1], P(('front', 'sub')), may hold values from 0 to 7; in each aligned block of 128 rows (0 to 127, 128 to 255, ...) at most 32 rows name the same one
- child_factors: float32 [16, 512, 512], P('front', 'sub'), as said below
- child_columns: int32 [16, 512], P('front'), may hold values from 0 to 1023, as said below
- damping: float32 [8, 1024], P('front'), may hold values from 0.5 to 2
Outputs:
- front_factor: float32 [8, 1024, 1024], P('front', 'sub')
Inputs may be any that keep to these rules, and one draw needn't show every extreme that they name: `front_of_row`: among the 128 rows of one device, at most 32 name the same front, and some device's block reaches this bound. `child_factors`: each block is upper triangular with a positive diagonal. `child_columns`: each row names 512 distinct columns.
All inputs are finite; a program needn't handle non-finite values.
Results may differ from a plain program's by a relative error of at most 0.0003.
Values sent between devices are 32-bit elements; how exact they have to be, the bound alone decides.
No kernel may reach another device: no remote copies, remote signals or barrier semaphores. Data moves between devices by JAX's collectives and lax.ppermute only.
A program may use at most 64 MiB of HBM per device.

v0:
```python
import functools

import jax
import jax.numpy as jnp
from jax import lax
from jax.experimental import pallas as pl
from jax.experimental.pallas import tpu as pltpu
from jax.sharding import PartitionSpec as P


HIGHEST = lax.Precision.HIGHEST


def cost(us):
    return pl.CostEstimate(flops=int(us * 5e8), bytes_accessed=0, transcendentals=0)


f32 = jnp.float32


def dot(a, b, ca=1, cb=0):
    return lax.dot_general(a, b, (((ca,), (cb,)), ((), ())), precision=HIGHEST, preferred_element_type=f32)


def rowb(v, j):
    return jnp.broadcast_to(v[j:j + 1, :], v.shape)


def factor_tile(x, store_r, store_w, spread_ref, n=128, width=16):
    lane = lax.broadcasted_iota(jnp.int32, (8, n), 1)
    sub = lax.broadcasted_iota(jnp.int32, (8, n), 0)
    lane1 = lax.broadcasted_iota(jnp.int32, (1, n), 1)
    per = width // 8
    blocks = n // width

    def spread(v, c, slot):
        spread_ref[slot] = jnp.broadcast_to(v[:, c:c + 1], v.shape)
        return spread_ref[slot]

    own = [x[8 * v:8 * v + 8, :] for v in range(per)]
    nxt = [x[width + 8 * v:width + 8 * v + 8, :] for v in range(per)]
    rest = x[2 * width:, :]
    for blk in range(blocks):
        lo = blk * width
        base = (blk % 2) * 2 * per * width
        t = list(own)
        w = [jnp.where(lane < lo, own[v], jnp.where(lane == sub + (lo + 8 * v), 1.0, 0.0)) for v in range(per)]
        b = [[None] * width for _ in range(per)]
        for c in range(width):
            for v in range(per):
                b[v][c] = spread(own[v], lo + c, base + v * width + c)
        last = blk == blocks - 1
        if not last:
            later = [[None] * width for _ in range(per)]
            for c in range(width):
                for v in range(per):
                    later[v][c] = spread(nxt[v], lo + c, base + (per + v) * width + c)
        for j in range(width):
            pv, jj = divmod(j, 8)
            here = sub == jj
            d = rowb(b[pv][j], jj)
            inv = 1.0 / d
            root = lax.rsqrt(d)
            cols = [b[v][j] for v in range(per)]
            cols[pv] = jnp.where(here, -1.0, cols[pv])
            for c in range(j + 1, width):
                row = rowb(b[pv][c], jj)
                if c == j + 1:
                    for v in range(per):
                        kept = jnp.where(here, 0.0, b[v][c]) if v == pv else b[v][c]
                        b[v][c] = kept - (cols[v] * row) * inv
                else:
                    row = row * inv
                    for v in range(per):
                        kept = jnp.where(here, 0.0, b[v][c]) if v == pv else b[v][c]
                        b[v][c] = kept - cols[v] * row
            trow, wrow = rowb(t[pv], jj), rowb(w[pv], jj)
            store_r(lo + j, jnp.where(lane1 >= lo + j, (trow * root)[0:1], 0.0))
            store_w(lo + j, (wrow * root)[0:1])
            tp, wp = trow * inv, wrow * inv
            for v in range(per):
                if last and v < pv:
                    continue
                for a, p in ((t, tp), (w, wp)):
                    kept = jnp.where(here, 0.0, a[v]) if v == pv else a[v]
                    a[v] = kept - cols[v] * p
        if last:
            break
        inside = (lane >= lo) & (lane < lo + width)
        z = [jnp.where(lane < lo + width, w[v], t[v]) for v in range(per)]
        new = []
        for v in range(per):
            terms = [later[v][c] * rowb(z[c // 8], c % 8) for c in range(width)]
            while len(terms) > 1:
                terms = [terms[q] + terms[q + 1] for q in range(0, len(terms), 2)]
            new.append(jnp.where(inside, 0.0, nxt[v]) - terms[0])
        own = new
        if rest.shape[0]:
            parts = [jnp.zeros((lo, n), f32)] if lo else []
            parts += z + [jnp.zeros((n - lo - width, n), f32)]
            zpad = jnp.concatenate(parts, axis=0)
            lane_r = lax.broadcasted_iota(jnp.int32, rest.shape, 1)
            rest = jnp.where((lane_r >= lo) & (lane_r < lo + width), 0.0, rest) - dot(rest, zpad)
            nxt = [rest[8 * v:8 * v + 8, :] for v in range(per)]
            rest = rest[width:, :]


def block_kernel(nprev, width, *refs):
    g_ref = refs[0]
    prev = refs[1:1 + nprev]
    r_ref, tile_ref, w_ref, spread_ref = refs[1 + nprev:]
    rows, cols = g_ref.shape
    half = w_ref.shape[0]
    u = g_ref[...]
    for t in range(nprev):
        off = rows * (nprev - t)
        u = u - dot(prev[t][:, off:off + rows], prev[t][:, off:], 0, 0)
    r_ref[...] = u

    def store_r(i, v):
        tile_ref[i:i + 1, :] = v

    def store_w(i, v):
        w_ref[i:i + 1, :] = v

    def panel(p, carry):
        for q in range(1, rows // half):

            @pl.when(p == q)
            def _():
                a = q * half
                done = dot(r_ref[0:a, a:a + half], r_ref[0:a, a:], 0, 0)
                r_ref[a:a + half, a:] = r_ref[a:a + half, a:] - done

        at = pl.ds(pl.multiple_of(p * half, half), half)
        factor_tile(r_ref[at, at], store_r, store_w, spread_ref, half, width)
        for q in range(rows // half):

            @pl.when(p == q)
            def _():
                a = q * half
                if a:
                    r_ref[a:a + half, 0:a] = jnp.zeros((half, a), f32)
                if a + half < cols:
                    r_ref[a:a + half, a + half:] = dot(w_ref[...], r_ref[a:a + half, a + half:])
                r_ref[a:a + half, a:a + half] = tile_ref[...]

        return carry

    lax.fori_loop(0, rows // half, panel, 0)


def chol_block(g, prev, width=16):
    n = len(prev)
    return pl.pallas_call(
        functools.partial(block_kernel, n, width),
        out_shape=jax.ShapeDtypeStruct(g.shape, f32),
        in_specs=[pl.BlockSpec(memory_space=pltpu.VMEM)] * (n + 1),
        out_specs=pl.BlockSpec(memory_space=pltpu.VMEM),
        scratch_shapes=[
            pltpu.VMEM((128, 128), f32),
            pltpu.VMEM((128, 128), f32),
            pltpu.VMEM((width * width // 2, 8, 128), f32),
        ],
        compiler_params=pltpu.CompilerParams(vmem_limit_bytes=12 << 20),
        cost_estimate=cost(6),
        name="factor_block",
    )(g, *prev)


def split3(x):
    high = x.astype(jnp.bfloat16)
    rest = x - high.astype(f32)
    mid = rest.astype(jnp.bfloat16)
    low = (rest - mid.astype(f32)).astype(jnp.bfloat16)
    return high, mid, low


def pick_exact(onehot, x, ca, cb, onehot_left):
    total = None
    for piece in split3(x):
        a, b = (onehot, piece) if onehot_left else (piece, onehot)
        part = lax.dot_general(a, b, (((ca,), (cb,)), ((), ())), preferred_element_type=f32)
        total = part if total is None else total + part
    return total


def route_kernel(capacity, rows_ref, row_ref, out_ref):
    n = rows_ref.shape[0]
    slots = out_ref.shape[0]
    down = lax.broadcasted_iota(jnp.int32, (n, n), 0)
    across = lax.broadcasted_iota(jnp.int32, (n, n), 1)
    row = row_ref[...].astype(f32)
    column = jnp.sum(jnp.where(down == across, jnp.broadcast_to(row, (n, n)), 0.0), axis=1, keepdims=True)
    earlier = (column == row) & (down < across)
    position = jnp.sum(jnp.where(earlier, 1.0, 0.0), axis=0, keepdims=True)
    slot = row_ref[...] * capacity + position.astype(jnp.int32)
    pick = lax.broadcasted_iota(jnp.int32, (slots, n), 0) == slot
    out_ref[...] = pick_exact(pick.astype(f32).astype(jnp.bfloat16), rows_ref[...], 1, 0, True)


def route(row_values, front_of_row, fronts):
    n, width = row_values.shape
    capacity = 2 * n // fronts
    return pl.pallas_call(
        functools.partial(route_kernel, capacity),
        out_shape=jax.ShapeDtypeStruct((fronts * capacity, width), f32),
        in_specs=[pl.BlockSpec(memory_space=pltpu.VMEM)] * 2,
        out_specs=pl.BlockSpec(memory_space=pltpu.VMEM),
        cost_estimate=cost(3),
        name="route",
    )(row_values, front_of_row.reshape(1, n))


def dot16(a, b, ca, cb):
    return lax.dot_general(a, b, (((ca,), (cb,)), ((), ())), preferred_element_type=f32)


def split2(x):
    high = x.astype(jnp.bfloat16)
    return high, (x - high.astype(f32)).astype(jnp.bfloat16)


def gram_block(high_ref, low_ref, lo, block):
    left_high, left_low = high_ref[:, lo:lo + block], low_ref[:, lo:lo + block]
    small = dot16(left_high, low_ref[:, lo:], 0, 0) + dot16(left_low, high_ref[:, lo:], 0, 0)
    return small + dot16(left_high, high_ref[:, lo:], 0, 0)


def children_kernel(block, nparts, *refs):
    parts = refs[:nparts]
    columns_ref, damping_ref, own_ref = refs[nparts:nparts + 3]
    outs = refs[nparts + 3:-3]
    stack_ref, high_ref, low_ref = refs[-3:]
    width = high_ref.shape[1]
    kids, rows, contrib = parts[0].shape
    each = rows * nparts
    for q in range(nparts):
        stack_ref[:, q * rows:(q + 1) * rows, :] = parts[q][...]
    high_ref[kids * each:, :], low_ref[kids * each:, :] = split2(own_ref[...])
    parent = lax.broadcasted_iota(jnp.int32, (width, contrib), 0)

    def place(c, carry):
        spread = (parent == columns_ref[pl.ds(c, 1), :]).astype(f32).astype(jnp.bfloat16)
        high, low = split2(stack_ref[c])
        at = pl.ds(pl.multiple_of(c * each, each), each)
        high_ref[at, :] = dot16(high, spread, 1, 1).astype(jnp.bfloat16)
        low_ref[at, :] = dot16(low, spread, 1, 1).astype(jnp.bfloat16)
        return carry

    lax.fori_loop(0, kids, place, 0)
    weight = damping_ref[...]
    for s, out_ref in enumerate(outs):
        lo = s * block
        down = lax.broadcasted_iota(jnp.int32, out_ref.shape, 0)
        across = lax.broadcasted_iota(jnp.int32, out_ref.shape, 1)
        diag = jnp.where(down == across, weight[:, lo:] * weight[:, lo:], 0.0)
        out_ref[...] = diag + gram_block(high_ref, low_ref, lo, block)


def block_shapes(width, block):
    return [jax.ShapeDtypeStruct((block, width - lo), f32) for lo in range(0, width, block)]


def children_gram(parts, columns, damping, own, block):
    width = damping.shape[1]
    kids, rows, contrib = parts[0].shape
    shapes = block_shapes(width, block)
    return pl.pallas_call(
        functools.partial(children_kernel, block, len(parts)),
        out_shape=shapes,
        in_specs=[pl.BlockSpec(memory_space=pltpu.VMEM)] * (len(parts) + 3),
        out_specs=[pl.BlockSpec(memory_space=pltpu.VMEM)] * len(shapes),
        scratch_shapes=[pltpu.VMEM((kids, rows * len(parts), contrib), f32)]
        + [pltpu.VMEM((kids * rows * len(parts) + own.shape[0], width), jnp.bfloat16)] * 2,
        compiler_params=pltpu.CompilerParams(vmem_limit_bytes=28 << 20),
        cost_estimate=cost(10),
        name="children_gram",
    )(*parts, columns, damping, own)


def rays_kernel(block, nblocks, nparts, *refs):
    grams = refs[:nblocks]
    parts = refs[nblocks:nblocks + nparts]
    outs = refs[nblocks + nparts:-2]
    high_ref, low_ref = refs[-2:]
    rows = parts[0].shape[0]
    for q, part in enumerate(parts):
        at = slice(q * rows, (q + 1) * rows)
        high_ref[at, :], low_ref[at, :] = split2(part[...])
    for s in range(nblocks):
        lo = s * block
        outs[s][...] = grams[s][...] + gram_block(high_ref, low_ref, lo, block)


def rays_gram(grams, parts, block):
    rows, width = parts[0].shape
    return pl.pallas_call(
        functools.partial(rays_kernel, block, len(grams), len(parts)),
        out_shape=[jax.ShapeDtypeStruct(g.shape, f32) for g in grams],
        in_specs=[pl.BlockSpec(memory_space=pltpu.VMEM)] * (len(grams) + len(parts)),
        out_specs=[pl.BlockSpec(memory_space=pltpu.VMEM)] * len(grams),
        scratch_shapes=[pltpu.VMEM((rows * len(parts), width), jnp.bfloat16)] * 2,
        compiler_params=pltpu.CompilerParams(vmem_limit_bytes=20 << 20),
        cost_estimate=cost(5),
        name="rays_gram",
    )(*grams, *parts)


AXES = ("front", "sub")


def leader_of(front, subs):
    return (subs // 2 - 1 + front % 2) % subs


def to_leader(x, fronts, subs):
    parts = [x]
    for j in range(subs - 1):
        pairs = []
        for f in range(fronts):
            leader = leader_of(f, subs)
            near = sorted((s for s in range(subs) if s != leader), key=lambda s: (abs(s - leader), s))
            pairs.append((f * subs + near[j], f * subs + leader))
        parts.append(lax.ppermute(x, AXES, pairs))
    return parts


def from_leader(x, owner, fronts, subs):
    pairs = [(f * subs + leader_of(f, subs), f * subs + owner) for f in range(fronts)]
    return lax.ppermute(x, AXES, pairs)


def local(row_values, front_of_row, child_factors, child_columns, damping):
    fronts, subs = lax.axis_size("front"), lax.axis_size("sub")
    width = row_values.shape[1]
    block = width // subs
    kid_parts = to_leader(child_factors, fronts, subs)
    outgoing = route(row_values, front_of_row, fronts)
    received = lax.all_to_all(outgoing, "front", split_axis=0, concat_axis=0, tiled=True)
    ray_parts = to_leader(received, fronts, subs)
    grams = children_gram(kid_parts, child_columns, damping, ray_parts[0], block)
    grams = rays_gram(grams, ray_parts[1:], block)
    factors, own = [], None
    for s in range(subs):
        factors.append(chol_block(grams[s], factors))
        sent = from_leader(factors[s], s, fronts, subs)
        sent = jnp.pad(sent, ((0, 0), (s * block, 0)))
        own = sent if own is None else own + sent
    return own[None]


def solution(mesh):
    in_specs = (
        P(("front", "sub"), None),
        P(("front", "sub"), None),
        P("front", "sub", None),
        P("front", None),
        P("front", None),
    )
    out_specs = P("front", "sub", None)

    return jax.shard_map(local, mesh=mesh, in_specs=in_specs, out_specs=out_specs, check_vma=False)
```

profile of v0, /device:TPU:27, one launch (start us, length us, event | category | flops | bytes accessed | tf_op | source)
XLA Modules:
  0.0 110.6 jit_solution(15228984275025894202)
XLA Ops:
  0.0 2.7 %route.1 = f32[256,1024]{1,0:T(8,128)} custom-call(f32[128,1024]{1,0:T(8,128)} %rows_ref.1, s32[1,128]{1,0:T(1,128)} %bitcast.10), custom_call_target="tpu_custom_call" | custom-call | flops 1500000000 | tf_op jit(solution)/shard_map/route/pallas_call | solution.py:205
  2.7 0.0 copy-start
  2.7 0.0 copy-start.1
  2.7 0.0 copy-start.2
  2.7 4.7 %all-to-all-start = ((f32[8,32,1024]{2,1,0:T(8,128)}), f32[8,32,1024]{2,1,0:T(8,128)S(1)}, u32[]{:S(2)}, u32[]{:S(2)}) async-start(f32[8,32,1024]{2,1,0:T(8,128)} %bitcast.9), calls=%async_computation | async-start | bytes 2097152 | tf_op jit(solution)/shard_map/all_to_all | solution.py:340
  7.3 0.0 copy-done
  7.3 2.1 %collective-permute-start.1 = (f32[2,128,512]{2,1,0:T(8,128)S(1)}, f32[2,128,512]{2,1,0:T(8,128)S(1)}, u32[]{:S(2)}, u32[]{:S(2)}) collective-permute-start(f32[2,128,512]{2,1,0:T(8,128)S(1)} %copy-done), channel_id=1, source_target_pairs={{2,1},{7,6},{10,9},{15,14},{18,17},{23,22},{26,25},{31,30}} | collective-permute-start | bytes 1572872 | tf_op jit(solution)/shard_map/ppermute | solution.py:325
  9.4 11.7 %all-to-all-done = f32[8,32,1024]{2,1,0:T(8,128)S(1)} async-done(((f32[8,32,1024]{2,1,0:T(8,128)}), f32[8,32,1024]{2,1,0:T(8,128)S(1)}, u32[]{:S(2)}, u32[]{:S(2)}) %all-to-all-start) | async-done | bytes 1048608 | tf_op jit(solution)/shard_map/all_to_all | solution.py:340
  21.1 0.7 collective-permute-start.5
  21.9 2.7 %collective-permute-start.4 = (f32[256,1024]{1,0:T(8,128)S(1)}, f32[256,1024]{1,0:T(8,128)S(1)}, u32[]{:S(2)}, u32[]{:S(2)}) collective-permute-start(f32[256,1024]{1,0:T(8,128)S(1)} %bitcast.6), channel_id=1, source_target_pairs={{2,1},{7,6},{10,9},{15,14},{18,17},{23,22},{26,25},{31,30}} | collective-permute-start | bytes 3145736 | tf_op jit(solution)/shard_map/ppermute | solution.py:325
  24.6 0.7 collective-permute-start.3
  25.3 0.7 collective-permute-start
  26.0 0.0 collective-permute-done.1.refs_2_
  26.0 0.7 collective-permute-start.2
  26.7 0.0 collective-permute-done.refs_1_
  26.7 0.0 collective-permute-done.2.refs_3_
  26.8 0.0 copy-done.1
  26.8 0.0 copy-done.2
  26.8 8.2 %children_gram.1 = (f32[256,1024]{1,0:T(8,128)S(1)}, f32[256,768]{1,0:T(8,128)S(1)}, f32[256,512]{1,0:T(8,128)S(1)}, f32[256,256]{1,0:T(8,128)S(1)}) custom-call(f32[2,128,512]{2,1,0:T(8,128)S(1)} %copy-done, f32[2,128,512]{2,1,0:T(8,128)S(1)} %collective-permute-done.refs_1_, f32[2,128,512]{2,1,0:T(8,128)S(1)} %collective-permute-done.1.refs_2_, ...), custom_call_target="tpu_custom_call" | custom-call | flops 5000000000 | tf_op jit(solution)/shard_map/children_gram/pallas_call | solution.py:269
  35.0 0.0 collective-permute-done.5.refs_6_
  35.0 12.5 %collective-permute-done.4.refs_5_ = f32[256,1024]{1,0:T(8,128)S(1)} collective-permute-done((f32[256,1024]{1,0:T(8,128)S(1)}, f32[256,1024]{1,0:T(8,128)S(1)}, u32[]{:S(2)}, u32[]{:S(2)}) %collective-permute-start.4) | collective-permute-done | bytes 1048608 | tf_op jit(solution)/shard_map/ppermute | solution.py:325
  47.5 0.0 collective-permute-done.3.refs_4_
  47.5 3.2 %rays_gram.1 = (f32[256,1024]{1,0:T(8,128)S(1)}, f32[256,768]{1,0:T(8,128)S(1)}, f32[256,512]{1,0:T(8,128)S(1)}, f32[256,256]{1,0:T(8,128)S(1)}) custom-call(f32[256,1024]{1,0:T(8,128)S(1)} %get-tuple-element.13.refs_0_, f32[256,768]{1,0:T(8,128)S(1)} %get-tuple-element.14.refs_1_, f32[256,512]{1,0:T(8,128)S(1)} %get-tuple-element.15.refs_2_, ...), custom_call_target="tpu_custom_call" | custom-call | flops 2500000000 | tf_op jit(solution)/shard_map/rays_gram/pallas_call | solution.py:298
  50.7 6.4 %factor_block.4.refs_1_ = f32[256,1024]{1,0:T(8,128)S(1)} custom-call(f32[256,1024]{1,0:T(8,128)S(1)} %get-tuple-element.17.refs_0_), custom_call_target="tpu_custom_call" | custom-call | flops 3000000000 | tf_op jit(solution)/shard_map/factor_block/pallas_call | solution.py:155
  57.2 0.9 collective-permute-start.6
  58.1 6.9 %factor_block.5.refs_2_ = f32[256,768]{1,0:T(8,128)S(1)} custom-call(f32[256,768]{1,0:T(8,128)S(1)} %get-tuple-element.18.refs_0_, f32[256,1024]{1,0:T(8,128)S(1)} %factor_block.4.refs_1_), custom_call_target="tpu_custom_call" | custom-call | flops 3000000000 | tf_op jit(solution)/shard_map/factor_block/pallas_call | solution.py:155
  64.9 0.7 collective-permute-start.7
  65.7 6.8 %factor_block.6.refs_3_ = f32[256,512]{1,0:T(8,128)S(1)} custom-call(f32[256,512]{1,0:T(8,128)S(1)} %get-tuple-element.19.refs_0_, f32[256,1024]{1,0:T(8,128)S(1)} %factor_block.4.refs_1_, f32[256,768]{1,0:T(8,128)S(1)} %factor_block.5.refs_2_), custom_call_target="tpu_custom_call" | custom-call | flops 3000000000 | tf_op jit(solution)/shard_map/factor_block/pallas_call | solution.py:155
  72.5 0.7 collective-permute-start.8
  73.2 6.1 %factor_block.7 = f32[256,256]{1,0:T(8,128)S(1)} custom-call(f32[256,256]{1,0:T(8,128)S(1)} %get-tuple-element.20.refs_0_, f32[256,1024]{1,0:T(8,128)S(1)} %factor_block.4.refs_1_, f32[256,768]{1,0:T(8,128)S(1)} %factor_block.5.refs_2_, f32[256,512]{1,0:T(8,128)S(1)} %factor_block.6.refs_3_), custom_call_target="tpu_custom_call" | custom-call | flops 3000000000 | tf_op jit(solution)/shard_map/factor_block/pallas_call | solution.py:155
  79.3 1.3 %collective-permute-start.9 = (f32[256,256]{1,0:T(8,128)S(1)}, f32[256,256]{1,0:T(8,128)S(1)}, u32[]{:S(2)}, u32[]{:S(2)}) collective-permute-start(f32[256,256]{1,0:T(8,128)S(1)} %factor_block.7), channel_id=1, source_target_pairs={{1,3},{6,7},{9,11},{14,15},{17,19},{22,23},{25,27},{30,31}} | collective-permute-start | bytes 786440 | tf_op jit(solution)/shard_map/ppermute | solution.py:331
  80.6 28.8 %collective-permute-done.9 = f32[256,256]{1,0:T(8,128)S(1)} collective-permute-done((f32[256,256]{1,0:T(8,128)S(1)}, f32[256,256]{1,0:T(8,128)S(1)}, u32[]{:S(2)}, u32[]{:S(2)}) %collective-permute-start.9) | collective-permute-done | bytes 262176 | tf_op jit(solution)/shard_map/ppermute | solution.py:331
  109.4 0.0 collective-permute-done.8
  109.4 0.0 collective-permute-done.7
  109.4 0.0 collective-permute-done.6
  109.4 1.2 %add_bitcast_fusion = f32[1,256,1024]{2,1,0:T(8,128)} fusion(f32[256,256]{1,0:T(8,128)S(1)} %collective-permute-done.9, f32[256,512]{1,0:T(8,128)S(1)} %collective-permute-done.8, f32[256,1024]{1,0:T(8,128)S(1)} %collective-permute-done.6, f32[256,768]{1,0:T(8,128)S(1)} %collective-permute-done.7), kind=kLoop, calls=%fused_computation | loop fusion | flops 786432 | bytes 3670016 | tf_op jit(solution)/shard_map/broadcast_in_dim | solution.py:350
Async XLA Ops:
  2.7 4.7 %copy-start = (f32[2,128,512]{2,1,0:T(8,128)S(1)}, f32[2,128,512]{2,1,0:T(8,128)}, u32[]{:S(2)}) copy-start(f32[2,128,512]{2,1,0:T(8,128)} %refs_0_.1) | copy-start | bytes 1572868
  2.7 24.1 %copy-start.1 = (s32[2,512]{1,0:T(2,128)S(1)}, s32[2,512]{1,0:T(2,128)}, u32[]{:S(2)}) copy-start(s32[2,512]{1,0:T(2,128)} %refs_4_.1) | copy-start | bytes 12292
  2.7 24.1 %copy-start.2 = (f32[1,1024]{1,0:T(1,128)S(1)}, f32[1,1024]{1,0:T(1,128)}, u32[]{:S(2)}) copy-start(f32[1,1024]{1,0:T(1,128)} %refs_5_.1) | copy-start | bytes 12292
  2.7 18.5 %all-to-all-start = ((f32[8,32,1024]{2,1,0:T(8,128)}), f32[8,32,1024]{2,1,0:T(8,128)S(1)}, u32[]{:S(2)}, u32[]{:S(2)}) async-start(f32[8,32,1024]{2,1,0:T(8,128)} %bitcast.9), calls=%async_computation | async-start | bytes 2097152 | tf_op jit(solution)/shard_map/all_to_all | solution.py:340
  7.3 18.7 %collective-permute-start.1 = (f32[2,128,512]{2,1,0:T(8,128)S(1)}, f32[2,128,512]{2,1,0:T(8,128)S(1)}, u32[]{:S(2)}, u32[]{:S(2)}) collective-permute-start(f32[2,128,512]{2,1,0:T(8,128)S(1)} %copy-done), channel_id=1, source_target_pairs={{2,1},{7,6},{10,9},{15,14},{18,17},{23,22},{26,25},{31,30}} | collective-permute-start | bytes 1572872 | tf_op jit(solution)/shard_map/ppermute | solution.py:325
  21.1 13.8 %collective-permute-start.5 = (f32[256,1024]{1,0:T(8,128)S(1)}, f32[256,1024]{1,0:T(8,128)S(1)}, u32[]{:S(2)}, u32[]{:S(2)}) collective-permute-start(f32[256,1024]{1,0:T(8,128)S(1)} %bitcast.5), channel_id=1, source_target_pairs={{3,1},{4,6},{11,9},{12,14},{19,17},{20,22},{27,25},{28,30}} | collective-permute-start | bytes 3145736 | tf_op jit(solution)/shard_map/ppermute | solution.py:325
  21.9 25.6 %collective-permute-start.4 = (f32[256,1024]{1,0:T(8,128)S(1)}, f32[256,1024]{1,0:T(8,128)S(1)}, u32[]{:S(2)}, u32[]{:S(2)}) collective-permute-start(f32[256,1024]{1,0:T(8,128)S(1)} %bitcast.6), channel_id=1, source_target_pairs={{2,1},{7,6},{10,9},{15,14},{18,17},{23,22},{26,25},{31,30}} | collective-permute-start | bytes 3145736 | tf_op jit(solution)/shard_map/ppermute | solution.py:325
  24.6 22.9 %collective-permute-start.3 = (f32[256,1024]{1,0:T(8,128)S(1)}, f32[256,1024]{1,0:T(8,128)S(1)}, u32[]{:S(2)}, u32[]{:S(2)}) collective-permute-start(f32[256,1024]{1,0:T(8,128)S(1)} %bitcast.7), channel_id=1, source_target_pairs={{0,1},{5,6},{8,9},{13,14},{16,17},{21,22},{24,25},{29,30}} | collective-permute-start | bytes 3145736 | tf_op jit(solution)/shard_map/ppermute | solution.py:325
  25.3 1.4 %collective-permute-start = (f32[2,128,512]{2,1,0:T(8,128)S(1)}, f32[2,128,512]{2,1,0:T(8,128)S(1)}, u32[]{:S(2)}, u32[]{:S(2)}) collective-permute-start(f32[2,128,512]{2,1,0:T(8,128)S(1)} %copy-done), channel_id=1, source_target_pairs={{0,1},{5,6},{8,9},{13,14},{16,17},{21,22},{24,25},{29,30}} | collective-permute-start | bytes 1572872 | tf_op jit(solution)/shard_map/ppermute | solution.py:325
  26.0 0.7 collective-permute-start.2
  57.2 52.2 %collective-permute-start.6 = (f32[256,1024]{1,0:T(8,128)S(1)}, f32[256,1024]{1,0:T(8,128)S(1)}, u32[]{:S(2)}, u32[]{:S(2)}) collective-permute-start(f32[256,1024]{1,0:T(8,128)S(1)} %factor_block.4.refs_1_), channel_id=1, source_target_pairs={{1,0},{6,4},{9,8},{14,12},{17,16},{22,20},{25,24},{30,28}} | collective-permute-start | bytes 3145736 | tf_op jit(solution)/shard_map/ppermute | solution.py:331
  64.9 44.4 %collective-permute-start.7 = (f32[256,768]{1,0:T(8,128)S(1)}, f32[256,768]{1,0:T(8,128)S(1)}, u32[]{:S(2)}, u32[]{:S(2)}) collective-permute-start(f32[256,768]{1,0:T(8,128)S(1)} %factor_block.5.refs_2_), channel_id=1, source_target_pairs={{1,1},{6,5},{9,9},{14,13},{17,17},{22,21},{25,25},{30,29}} | collective-permute-start | bytes 2359304 | tf_op jit(solution)/shard_map/ppermute | solution.py:331
  72.5 36.9 %collective-permute-start.8 = (f32[256,512]{1,0:T(8,128)S(1)}, f32[256,512]{1,0:T(8,128)S(1)}, u32[]{:S(2)}, u32[]{:S(2)}) collective-permute-start(f32[256,512]{1,0:T(8,128)S(1)} %factor_block.6.refs_3_), channel_id=1, source_target_pairs={{1,2},{6,6},{9,10},{14,14},{17,18},{22,22},{25,26},{30,30}} | collective-permute-start | bytes 1572872 | tf_op jit(solution)/shard_map/ppermute | solution.py:331
  79.3 30.1 %collective-permute-start.9 = (f32[256,256]{1,0:T(8,128)S(1)}, f32[256,256]{1,0:T(8,128)S(1)}, u32[]{:S(2)}, u32[]{:S(2)}) collective-permute-start(f32[256,256]{1,0:T(8,128)S(1)} %factor_block.7), channel_id=1, source_target_pairs={{1,3},{6,7},{9,11},{14,15},{17,19},{22,23},{25,27},{30,31}} | collective-permute-start | bytes 786440 | tf_op jit(solution)/shard_map/ppermute | solution.py:331
where the time goes:
time: 111 us
  waiting for transfers between devices  53 us (48%)
  Pallas kernels  40.3 us (36%)
  starting transfers between devices  15.9 us (14%)
  other arithmetic  1.16 us (1%)
    ppermute x4, waiting for transfers between devices, from_leader(): return lax.ppermute(x, AXES, pairs)  28.8 us
    pallas_call x4, Pallas kernels, chol_block(): pl.pallas_call(functools.partial(block_kernel, n, width), out_shape=jax.S...  26.2 us
    ppermute x6, waiting for transfers between devices, to_leader(): parts.append(lax.ppermute(x, AXES, pairs))  12.5 us
    all_to_all x1, waiting for transfers between devices, local(): lax.all_to_all(outgoing, 'front', split_axis=0, concat_axis=0, tiled=True)  11.7 us
    pallas_call x1, Pallas kernels, children_gram(): pl.pallas_call(functools.partial(children_kernel, block, len(parts)), out...  8.19 us
    ppermute x6, starting transfers between devices, to_leader(): parts.append(lax.ppermute(x, AXES, pairs))  7.63 us
    all_to_all x1, starting transfers between devices, local(): lax.all_to_all(outgoing, 'front', split_axis=0, concat_axis=0, tiled=True)  4.67 us
    ppermute x4, starting transfers between devices, from_leader(): return lax.ppermute(x, AXES, pairs)  3.61 us
  transfers between devices with their start and end apart: 11, of which 3 were waited for; matrix products, arithmetic and copies ran while one was open for 0% of the time, Pallas kernels for 25%

commit v1 on v0

--- a/solution.py
+++ b/solution.py
@@ -9,6 +9,8 @@
 
 
 HIGHEST = lax.Precision.HIGHEST
+TILE = 128
+AXES = ("front", "sub")
 
 
 def cost(us):
@@ -18,8 +20,36 @@
 f32 = jnp.float32
 
 
+def leader_of(front, subs):
+    return (subs // 2 - 1 + front % 2) % subs
+
+
+def on_leader(body, *refs):
+    @pl.when(lax.axis_index("sub") == leader_of(lax.axis_index("front"), lax.axis_size("sub")))
+    def _():
+        body(*refs)
+
+
 def dot(a, b, ca=1, cb=0):
     return lax.dot_general(a, b, (((ca,), (cb,)), ((), ())), precision=HIGHEST, preferred_element_type=f32)
+
+
+def dot16(a, b, ca, cb):
+    return lax.dot_general(a, b, (((ca,), (cb,)), ((), ())), preferred_element_type=f32)
+
+
+def split2(x):
+    high = x.astype(jnp.bfloat16)
+    return high, (x - high.astype(f32)).astype(jnp.bfloat16)
+
+
+def pair_dot(a, b, ca, cb):
+    small = dot16(a[0], b[1], ca, cb) + dot16(a[1], b[0], ca, cb)
+    return small + dot16(a[0], b[0], ca, cb)
+
+
+def dot3(a, b, ca=1, cb=0):
+    return pair_dot(split2(a), split2(b), ca, cb)
 
 
 def rowb(v, j):
@@ -105,17 +135,9 @@
             rest = rest[width:, :]
 
 
-def block_kernel(nprev, width, *refs):
-    g_ref = refs[0]
-    prev = refs[1:1 + nprev]
-    r_ref, tile_ref, w_ref, spread_ref = refs[1 + nprev:]
-    rows, cols = g_ref.shape
+def factor_loop(r_ref, tile_ref, w_ref, spread_ref, width, keep=None):
+    rows, cols = r_ref.shape
     half = w_ref.shape[0]
-    u = g_ref[...]
-    for t in range(nprev):
-        off = rows * (nprev - t)
-        u = u - dot(prev[t][:, off:off + rows], prev[t][:, off:], 0, 0)
-    r_ref[...] = u
 
     def store_r(i, v):
         tile_ref[i:i + 1, :] = v
@@ -129,11 +151,13 @@
             @pl.when(p == q)
             def _():
                 a = q * half
-                done = dot(r_ref[0:a, a:a + half], r_ref[0:a, a:], 0, 0)
+                done = dot3(r_ref[0:a, a:a + half], r_ref[0:a, a:], 0, 0)
                 r_ref[a:a + half, a:] = r_ref[a:a + half, a:] - done
 
         at = pl.ds(pl.multiple_of(p * half, half), half)
         factor_tile(r_ref[at, at], store_r, store_w, spread_ref, half, width)
+        if keep is not None:
+            keep[at, :] = w_ref[...]
         for q in range(rows // half):
 
             @pl.when(p == q)
@@ -142,26 +166,43 @@
                 if a:
                     r_ref[a:a + half, 0:a] = jnp.zeros((half, a), f32)
                 if a + half < cols:
-                    r_ref[a:a + half, a + half:] = dot(w_ref[...], r_ref[a:a + half, a + half:])
+                    r_ref[a:a + half, a + half:] = dot3(w_ref[...], r_ref[a:a + half, a + half:])
                 r_ref[a:a + half, a:a + half] = tile_ref[...]
 
         return carry
 
     lax.fori_loop(0, rows // half, panel, 0)
+
+
+def block_kernel(nprev, width, *refs):
+    g_ref = refs[0]
+    prev = refs[1:1 + nprev]
+    r_ref = refs[1 + nprev]
+    rows = g_ref.shape[0]
+    u = g_ref[...]
+    for t in range(nprev):
+        off = rows * (nprev - t)
+        u = u - dot3(prev[t][:, off:off + rows], prev[t][:, off:], 0, 0)
+    r_ref[...] = u
+    factor_loop(*refs[1 + nprev:], width)
+
+
+def factor_scratch(width):
+    return [
+        pltpu.VMEM((TILE, TILE), f32),
+        pltpu.VMEM((TILE, TILE), f32),
+        pltpu.VMEM((width * width // 2, 8, TILE), f32),
+    ]
 
 
 def chol_block(g, prev, width=16):
     n = len(prev)
     return pl.pallas_call(
-        functools.partial(block_kernel, n, width),
+        functools.partial(on_leader, functools.partial(block_kernel, n, width)),
         out_shape=jax.ShapeDtypeStruct(g.shape, f32),
         in_specs=[pl.BlockSpec(memory_space=pltpu.VMEM)] * (n + 1),
         out_specs=pl.BlockSpec(memory_space=pltpu.VMEM),
-        scratch_shapes=[
-            pltpu.VMEM((128, 128), f32),
-            pltpu.VMEM((128, 128), f32),
-            pltpu.VMEM((width * width // 2, 8, 128), f32),
-        ],
+        scratch_shapes=factor_scratch(width),
         compiler_params=pltpu.CompilerParams(vmem_limit_bytes=12 << 20),
         cost_estimate=cost(6),
         name="factor_block",
@@ -185,9 +226,9 @@
     return total
 
 
-def route_kernel(capacity, rows_ref, row_ref, out_ref):
+def route_kernel(capacity, rows_ref, row_ref, *out_refs):
     n = rows_ref.shape[0]
-    slots = out_ref.shape[0]
+    slots, width = out_refs[0].shape
     down = lax.broadcasted_iota(jnp.int32, (n, n), 0)
     across = lax.broadcasted_iota(jnp.int32, (n, n), 1)
     row = row_ref[...].astype(f32)
@@ -196,7 +237,9 @@
     position = jnp.sum(jnp.where(earlier, 1.0, 0.0), axis=0, keepdims=True)
     slot = row_ref[...] * capacity + position.astype(jnp.int32)
     pick = lax.broadcasted_iota(jnp.int32, (slots, n), 0) == slot
-    out_ref[...] = pick_exact(pick.astype(f32).astype(jnp.bfloat16), rows_ref[...], 1, 0, True)
+    pick = pick.astype(f32).astype(jnp.bfloat16)
+    for h, out_ref in enumerate(out_refs):
+        out_ref[...] = pick_exact(pick, rows_ref[:, h * width:(h + 1) * width], 1, 0, True)
 
 
 def route(row_values, front_of_row, fronts):
@@ -204,40 +247,29 @@
     capacity = 2 * n // fronts
     return pl.pallas_call(
         functools.partial(route_kernel, capacity),
-        out_shape=jax.ShapeDtypeStruct((fronts * capacity, width), f32),
+        out_shape=[jax.ShapeDtypeStruct((fronts * capacity, width // 2), f32)] * 2,
         in_specs=[pl.BlockSpec(memory_space=pltpu.VMEM)] * 2,
-        out_specs=pl.BlockSpec(memory_space=pltpu.VMEM),
+        out_specs=[pl.BlockSpec(memory_space=pltpu.VMEM)] * 2,
         cost_estimate=cost(3),
         name="route",
     )(row_values, front_of_row.reshape(1, n))
 
 
-def dot16(a, b, ca, cb):
-    return lax.dot_general(a, b, (((ca,), (cb,)), ((), ())), preferred_element_type=f32)
-
-
-def split2(x):
-    high = x.astype(jnp.bfloat16)
-    return high, (x - high.astype(f32)).astype(jnp.bfloat16)
-
-
 def gram_block(high_ref, low_ref, lo, block):
-    left_high, left_low = high_ref[:, lo:lo + block], low_ref[:, lo:lo + block]
-    small = dot16(left_high, low_ref[:, lo:], 0, 0) + dot16(left_low, high_ref[:, lo:], 0, 0)
-    return small + dot16(left_high, high_ref[:, lo:], 0, 0)
+    left = high_ref[:, lo:lo + block], low_ref[:, lo:lo + block]
+    return pair_dot(left, (high_ref[:, lo:], low_ref[:, lo:]), 0, 0)
 
 
 def children_kernel(block, nparts, *refs):
     parts = refs[:nparts]
-    columns_ref, damping_ref, own_ref = refs[nparts:nparts + 3]
-    outs = refs[nparts + 3:-3]
+    columns_ref, damping_ref = refs[nparts:nparts + 2]
+    outs = refs[nparts + 2:-3]
     stack_ref, high_ref, low_ref = refs[-3:]
     width = high_ref.shape[1]
     kids, rows, contrib = parts[0].shape
     each = rows * nparts
     for q in range(nparts):
         stack_ref[:, q * rows:(q + 1) * rows, :] = parts[q][...]
-    high_ref[kids * each:, :], low_ref[kids * each:, :] = split2(own_ref[...])
     parent = lax.broadcasted_iota(jnp.int32, (width, contrib), 0)
 
     def place(c, carry):
@@ -262,56 +294,121 @@
     return [jax.ShapeDtypeStruct((block, width - lo), f32) for lo in range(0, width, block)]
 
 
-def children_gram(parts, columns, damping, own, block):
+def children_gram(parts, columns, damping, block):
     width = damping.shape[1]
     kids, rows, contrib = parts[0].shape
     shapes = block_shapes(width, block)
     return pl.pallas_call(
-        functools.partial(children_kernel, block, len(parts)),
+        functools.partial(on_leader, functools.partial(children_kernel, block, len(parts))),
         out_shape=shapes,
-        in_specs=[pl.BlockSpec(memory_space=pltpu.VMEM)] * (len(parts) + 3),
+        in_specs=[pl.BlockSpec(memory_space=pltpu.VMEM)] * (len(parts) + 2),
         out_specs=[pl.BlockSpec(memory_space=pltpu.VMEM)] * len(shapes),
         scratch_shapes=[pltpu.VMEM((kids, rows * len(parts), contrib), f32)]
-        + [pltpu.VMEM((kids * rows * len(parts) + own.shape[0], width), jnp.bfloat16)] * 2,
+        + [pltpu.VMEM((kids * rows * len(parts), width), jnp.bfloat16)] * 2,
         compiler_params=pltpu.CompilerParams(vmem_limit_bytes=28 << 20),
         cost_estimate=cost(10),
         name="children_gram",
-    )(*parts, columns, damping, own)
-
-
-def rays_kernel(block, nblocks, nparts, *refs):
-    grams = refs[:nblocks]
-    parts = refs[nblocks:nblocks + nparts]
-    outs = refs[nblocks + nparts:-2]
-    high_ref, low_ref = refs[-2:]
+    )(*parts, columns, damping)
+
+
+def split_parts(parts, high_ref, low_ref):
     rows = parts[0].shape[0]
     for q, part in enumerate(parts):
         at = slice(q * rows, (q + 1) * rows)
         high_ref[at, :], low_ref[at, :] = split2(part[...])
-    for s in range(nblocks):
+
+
+def lead_kernel(nlead, nparts, width, *refs):
+    grams = refs[:nlead]
+    parts = refs[nlead:nlead + nparts]
+    lead_ref, top_ref, keep_ref, high_ref, low_ref = refs[nlead + nparts:nlead + nparts + 5]
+    scratch = refs[nlead + nparts + 5:]
+    block = grams[0].shape[0]
+    cols = lead_ref.shape[1]
+    split_parts(parts, high_ref, low_ref)
+    for s in range(nlead):
         lo = s * block
-        outs[s][...] = grams[s][...] + gram_block(high_ref, low_ref, lo, block)
-
-
-def rays_gram(grams, parts, block):
-    rows, width = parts[0].shape
+        lead_ref[lo:lo + block, lo:] = grams[s][:, 0:cols - lo] + gram_block(high_ref, low_ref, lo, block)
+    factor_loop(lead_ref, *scratch, width, keep_ref)
+    top_ref[...] = lead_ref[0:block, :]
+
+
+def lead_factor(grams, parts, width=16):
+    block = grams[0].shape[0]
+    rows, cols = parts[0].shape
+    nlead = cols // block
+    ins = [*grams[:nlead], *parts]
     return pl.pallas_call(
-        functools.partial(rays_kernel, block, len(grams), len(parts)),
-        out_shape=[jax.ShapeDtypeStruct(g.shape, f32) for g in grams],
-        in_specs=[pl.BlockSpec(memory_space=pltpu.VMEM)] * (len(grams) + len(parts)),
-        out_specs=[pl.BlockSpec(memory_space=pltpu.VMEM)] * len(grams),
-        scratch_shapes=[pltpu.VMEM((rows * len(parts), width), jnp.bfloat16)] * 2,
+        functools.partial(on_leader, functools.partial(lead_kernel, nlead, len(parts), width)),
+        out_shape=[
+            jax.ShapeDtypeStruct((cols, cols), f32),
+            jax.ShapeDtypeStruct((block, cols), f32),
+            jax.ShapeDtypeStruct((cols, TILE), f32),
+            jax.ShapeDtypeStruct((rows * len(parts), cols), jnp.bfloat16),
+            jax.ShapeDtypeStruct((rows * len(parts), cols), jnp.bfloat16),
+        ],
+        in_specs=[pl.BlockSpec(memory_space=pltpu.VMEM)] * len(ins),
+        out_specs=[pl.BlockSpec(memory_space=pltpu.VMEM)] * 5,
+        scratch_shapes=factor_scratch(width),
         compiler_params=pltpu.CompilerParams(vmem_limit_bytes=20 << 20),
-        cost_estimate=cost(5),
-        name="rays_gram",
-    )(*grams, *parts)
-
-
-AXES = ("front", "sub")
-
-
-def leader_of(front, subs):
-    return (subs // 2 - 1 + front % 2) % subs
+        cost_estimate=cost(14),
+        name="lead_factor",
+    )(*ins)
+
+
+def cross_kernel(nblocks, nlead, nparts, *refs):
+    grams = refs[:nblocks]
+    parts = refs[nblocks:nblocks + nparts]
+    lead_ref, keep_ref, high1_ref, low1_ref = refs[nblocks + nparts:nblocks + nparts + 4]
+    outs = refs[nblocks + nparts + 4:-3]
+    x_ref, high_ref, low_ref = refs[-3:]
+    block = grams[0].shape[0]
+    cols = lead_ref.shape[1]
+    split_parts(parts, high_ref, low_ref)
+    right = high_ref[...], low_ref[...]
+    for s in range(nlead):
+        at = slice(s * block, (s + 1) * block)
+        left = high1_ref[:, at], low1_ref[:, at]
+        x_ref[at, :] = grams[s][:, cols - s * block:] + pair_dot(left, right, 0, 0)
+    for a in range(0, cols, TILE):
+        at = slice(a, a + TILE)
+        u = x_ref[at, :]
+        if a:
+            u = u - dot3(lead_ref[0:a, at], x_ref[0:a, :], 0, 0)
+        x_ref[at, :] = dot3(keep_ref[at, :], u)
+    for s in range(nlead):
+        at = slice(s * block, (s + 1) * block)
+        if s:
+            outs[s][:, 0:cols - s * block] = lead_ref[at, s * block:]
+            outs[s][:, cols - s * block:] = x_ref[at, :]
+        else:
+            outs[s][...] = x_ref[at, :]
+    high1, low1 = split2(x_ref[...])
+    for s in range(nlead, nblocks):
+        lo = (s - nlead) * block
+        left = high1[:, lo:lo + block], low1[:, lo:lo + block]
+        done = pair_dot(left, (high1[:, lo:], low1[:, lo:]), 0, 0)
+        outs[s][...] = grams[s][...] + gram_block(high_ref, low_ref, lo, block) - done
+
+
+def cross_update(grams, parts, lead, keep, high1, low1):
+    block = grams[0].shape[0]
+    rows, cols = parts[0].shape
+    nlead = cols // block
+    ins = [*grams, *parts, lead, keep, high1, low1]
+    shapes = [jax.ShapeDtypeStruct(g.shape, f32) for g in grams]
+    shapes[0] = jax.ShapeDtypeStruct((block, grams[0].shape[1] - cols), f32)
+    tall = (rows * len(parts), cols)
+    return pl.pallas_call(
+        functools.partial(on_leader, functools.partial(cross_kernel, len(grams), nlead, len(parts))),
+        out_shape=shapes,
+        in_specs=[pl.BlockSpec(memory_space=pltpu.VMEM)] * len(ins),
+        out_specs=[pl.BlockSpec(memory_space=pltpu.VMEM)] * len(shapes),
+        scratch_shapes=[pltpu.VMEM((cols, cols), f32)] + [pltpu.VMEM(tall, jnp.bfloat16)] * 2,
+        compiler_params=pltpu.CompilerParams(vmem_limit_bytes=28 << 20),
+        cost_estimate=cost(9),
+        name="cross_update",
+    )(*ins)
 
 
 def to_leader(x, fronts, subs):
@@ -336,18 +433,29 @@
     width = row_values.shape[1]
     block = width // subs
     kid_parts = to_leader(child_factors, fronts, subs)
-    outgoing = route(row_values, front_of_row, fronts)
-    received = lax.all_to_all(outgoing, "front", split_axis=0, concat_axis=0, tiled=True)
-    ray_parts = to_leader(received, fronts, subs)
-    grams = children_gram(kid_parts, child_columns, damping, ray_parts[0], block)
-    grams = rays_gram(grams, ray_parts[1:], block)
-    factors, own = [], None
-    for s in range(subs):
-        factors.append(chol_block(grams[s], factors))
-        sent = from_leader(factors[s], s, fronts, subs)
-        sent = jnp.pad(sent, ((0, 0), (s * block, 0)))
-        own = sent if own is None else own + sent
-    return own[None]
+    halves = []
+    for outgoing in route(row_values, front_of_row, fronts):
+        received = lax.all_to_all(outgoing, "front", split_axis=0, concat_axis=0, tiled=True)
+        halves.append(to_leader(received, fronts, subs))
+    grams = children_gram(kid_parts, child_columns, damping, block)
+    lead, top, keep, high1, low1 = lead_factor(grams, halves[0])
+    pieces = []
+
+    def send(x, owner, at):
+        sent = from_leader(x, owner, fronts, subs)
+        pieces.append(jnp.pad(sent, ((0, 0), (at, width - at - x.shape[1]))))
+
+    nlead = subs // 2
+    send(top, 0, 0)
+    rest = cross_update(grams, halves[1], lead, keep, high1, low1)
+    send(rest[0], 0, nlead * block)
+    for s in range(1, nlead):
+        send(rest[s], s, s * block)
+    factors = []
+    for s in range(nlead, subs):
+        factors.append(chol_block(rest[s], factors))
+        send(factors[-1], s, s * block)
+    return functools.reduce(jnp.add, pieces)[None]
 
 
 def solution(mesh):

time: 111 us -> 97.6 us (0.88)
  the two profiles are of different devices: /device:TPU:27 before, /device:TPU:0 now
where the time goes in v1:
time: 97.6 us; the launch traced here: 97 us
  waiting for transfers between devices  51 us (52%)
  starting transfers between devices  39.9 us (41%)
  Pallas kernels  4.8 us (5%)
  other arithmetic  1.16 us (1%)
    ppermute x5, waiting for transfers between devices, from_leader(): return lax.ppermute(x, AXES, pairs)  39.4 us
    ppermute x9, starting transfers between devices, to_leader(): parts.append(lax.ppermute(x, AXES, pairs))  26.3 us
    all_to_all x2, starting transfers between devices, local(): lax.all_to_all(outgoing, 'front', split_axis=0, concat_axis=0, tiled=True)  8.96 us
    all_to_all x2, waiting for transfers between devices, local(): lax.all_to_all(outgoing, 'front', split_axis=0, concat_axis=0, tiled=True)  6.16 us
    ppermute x9, waiting for transfers between devices, to_leader(): parts.append(lax.ppermute(x, AXES, pairs))  5.44 us
    ppermute x5, starting transfers between devices, from_leader(): return lax.ppermute(x, AXES, pairs)  4.65 us
    pallas_call x1, Pallas kernels, route(): pl.pallas_call(functools.partial(route_kernel, capacity), out_shape=[jax....  2.5 us
  transfers between devices with their start and end apart: 16, of which 5 were waited for; matrix products, arithmetic and copies ran while one was open for 0% of the time, Pallas kernels for 2%

profile of v1, /device:TPU:0, one launch (start us, length us, event | category | flops | bytes accessed | tf_op | source)
XLA Modules:
  0.0 97.0 jit_solution(8308484135880346135)
XLA Ops:
  0.0 2.5 %route.1 = (f32[256,512]{1,0:T(8,128)}, f32[256,512]{1,0:T(8,128)}) custom-call(f32[128,1024]{1,0:T(8,128)} %rows_ref.1, s32[1,128]{1,0:T(1,128)} %bitcast.16), custom_call_target="tpu_custom_call" | custom-call | flops 1500000000 | tf_op jit(solution)/shard_map/route/pallas_call | solution.py:248
  2.5 0.0 copy-start
  2.5 5.3 %all-to-all-start = ((f32[8,32,512]{2,1,0:T(8,128)}), f32[8,32,512]{2,1,0:T(8,128)S(1)}, u32[]{:S(2)}, u32[]{:S(2)}) async-start(f32[8,32,512]{2,1,0:T(8,128)} %bitcast.15), calls=%async_computation | async-start | bytes 1048576 | tf_op jit(solution)/shard_map/all_to_all | solution.py:438
  7.8 0.0 copy-done
  7.8 0.7 collective-permute-start.1
  8.5 4.1 %collective-permute-start = (f32[2,128,512]{2,1,0:T(8,128)S(1)}, f32[2,128,512]{2,1,0:T(8,128)S(1)}, u32[]{:S(2)}, u32[]{:S(2)}) collective-permute-start(f32[2,128,512]{2,1,0:T(8,128)S(1)} %copy-done), channel_id=1, source_target_pairs={{0,1},{5,6},{8,9},{13,14},{16,17},{21,22},{24,25},{29,30}} | collective-permute-start | bytes 1572872 | tf_op jit(solution)/shard_map/ppermute | solution.py:422
  12.7 1.5 %collective-permute-start.2 = (f32[2,128,512]{2,1,0:T(8,128)S(1)}, f32[2,128,512]{2,1,0:T(8,128)}, u32[]{:S(2)}, u32[]{:S(2)}) collective-permute-start(f32[2,128,512]{2,1,0:T(8,128)S(1)} %copy-done), channel_id=1, source_target_pairs={{3,1},{4,6},{11,9},{12,14},{19,17},{20,22},{27,25},{28,30}} | collective-permute-start | bytes 1572872 | tf_op jit(solution)/shard_map/ppermute | solution.py:422
  14.1 3.4 %all-to-all-done = f32[8,32,512]{2,1,0:T(8,128)S(1)} async-done(((f32[8,32,512]{2,1,0:T(8,128)}), f32[8,32,512]{2,1,0:T(8,128)S(1)}, u32[]{:S(2)}, u32[]{:S(2)}) %all-to-all-start) | async-done | bytes 524320 | tf_op jit(solution)/shard_map/all_to_all | solution.py:438
  17.5 0.0 copy-start.1
  17.5 0.0 copy-start.2
  17.6 3.6 %all-to-all-start.1 = ((f32[8,32,512]{2,1,0:T(8,128)}), f32[8,32,512]{2,1,0:T(8,128)S(1)}, u32[]{:S(2)}, u32[]{:S(2)}) async-start(f32[8,32,512]{2,1,0:T(8,128)} %bitcast.3), calls=%async_computation.1 | async-start | bytes 1048576 | tf_op jit(solution)/shard_map/all_to_all | solution.py:438
  21.2 0.7 collective-permute-start.5
  21.9 1.5 %collective-permute-start.4 = (f32[256,512]{1,0:T(8,128)S(1)}, f32[256,512]{1,0:T(8,128)}, u32[]{:S(2)}, u32[]{:S(2)}) collective-permute-start(f32[256,512]{1,0:T(8,128)S(1)} %bitcast.8), channel_id=1, source_target_pairs={{2,1},{7,6},{10,9},{15,14},{18,17},{23,22},{26,25},{31,30}} | collective-permute-start | bytes 1572872 | tf_op jit(solution)/shard_map/ppermute | solution.py:422
  23.4 0.0 collective-permute-done.1.refs_2_
  23.4 4.7 %collective-permute-start.3 = (f32[256,512]{1,0:T(8,128)S(1)}, f32[256,512]{1,0:T(8,128)}, u32[]{:S(2)}, u32[]{:S(2)}) collective-permute-start(f32[256,512]{1,0:T(8,128)S(1)} %bitcast.9), channel_id=1, source_target_pairs={{0,1},{5,6},{8,9},{13,14},{16,17},{21,22},{24,25},{29,30}} | collective-permute-start | bytes 1572872 | tf_op jit(solution)/shard_map/ppermute | solution.py:422
  28.1 2.8 %all-to-all-done.1 = f32[8,32,512]{2,1,0:T(8,128)S(1)} async-done(((f32[8,32,512]{2,1,0:T(8,128)}), f32[8,32,512]{2,1,0:T(8,128)S(1)}, u32[]{:S(2)}, u32[]{:S(2)}) %all-to-all-start.1) | async-done | bytes 524320 | tf_op jit(solution)/shard_map/all_to_all | solution.py:438
  30.8 0.0 collective-permute-done.refs_1_
  30.8 0.7 collective-permute-start.9
  31.5 0.0 collective-permute-done.2.refs_3_
  31.5 0.7 collective-permute-start.8
  32.2 0.0 copy-done.1
  32.2 0.0 copy-done.2
  32.3 1.0 %children_gram.1 = (f32[256,1024]{1,0:T(8,128)S(1)}, f32[256,768]{1,0:T(8,128)S(1)}, f32[256,512]{1,0:T(8,128)S(1)}, f32[256,256]{1,0:T(8,128)S(1)}) custom-call(f32[2,128,512]{2,1,0:T(8,128)S(1)} %copy-done, f32[2,128,512]{2,1,0:T(8,128)S(1)} %collective-permute-done.refs_1_, f32[2,128,512]{2,1,0:T(8,128)S(1)} %collective-permute-done.1.refs_2_, ...), custom_call_target="tpu_custom_call" | custom-call | flops 5000000000 | tf_op jit(solution)/shard_map/children_gram/pallas_call | solution.py:301
  33.3 0.0 collective-permute-done.5.refs_5_
  33.3 11.8 %collective-permute-start.7 = (f32[256,512]{1,0:T(8,128)S(1)}, f32[256,512]{1,0:T(8,128)S(1)}, u32[]{:S(2)}, u32[]{:S(2)}) collective-permute-start(f32[256,512]{1,0:T(8,128)S(1)} %bitcast.13), channel_id=1, source_target_pairs={{0,1},{5,6},{8,9},{13,14},{16,17},{21,22},{24,25},{29,30}} | collective-permute-start | bytes 1572872 | tf_op jit(solution)/shard_map/ppermute | solution.py:422
  45.1 0.0 collective-permute-done.4.refs_4_
  45.1 0.0 collective-permute-done.3.refs_3_
  45.1 1.2 %lead_factor.1 = (f32[512,512]{1,0:T(8,128)S(1)}, f32[256,512]{1,0:T(8,128)S(1)}, f32[512,128]{1,0:T(8,128)S(1)}, bf16[1024,512]{1,0:T(8,128)(2,1)S(1)}, bf16[1024,512]{1,0:T(8,128)(2,1)S(1)}) custom-call(f32[256,1024]{1,0:T(8,128)S(1)} %get-tuple-element.20.refs_0_, f32[256,768]{1,0:T(8,128)S(1)} %get-tuple-element.21.refs_1_, f32[256,512]{1,0:T(8,128)S(1)} %bitcast.10, ...), custom_call_target="tpu_custom_call" | custom-call | flops 7000000000 | tf_op jit(solution)/shard_map/lead_factor/pallas_call | solution.py:341
  46.3 0.0 collective-permute-done.9.refs_7_
  46.3 0.0 collective-permute-done.8.refs_6_
  46.3 5.4 %collective-permute-done.7.refs_5_ = f32[256,512]{1,0:T(8,128)S(1)} collective-permute-done((f32[256,512]{1,0:T(8,128)S(1)}, f32[256,512]{1,0:T(8,128)S(1)}, u32[]{:S(2)}, u32[]{:S(2)}) %collective-permute-start.7) | collective-permute-done | bytes 524320 | tf_op jit(solution)/shard_map/ppermute | solution.py:422
  51.7 0.7 collective-permute-start.11
  52.5 0.7 collective-permute-start.12
  53.2 1.3 %collective-permute-start.10 = (f32[256,512]{1,0:T(8,128)S(1)}, f32[256,512]{1,0:T(8,128)S(1)}, u32[]{:S(2)}, u32[]{:S(2)}) collective-permute-start(f32[256,512]{1,0:T(8,128)S(1)} %get-tuple-element.31), channel_id=1, source_target_pairs={{1,0},{6,4},{9,8},{14,12},{17,16},{22,20},{25,24},{30,28}} | collective-permute-start | bytes 1572872 | tf_op jit(solution)/shard_map/ppermute | solution.py:428
  54.5 1.3 %collective-permute-start.6 = (f32[256,512]{1,0:T(8,128)S(1)}, f32[256,512]{1,0:T(8,128)S(1)}, u32[]{:S(2)}, u32[]{:S(2)}) collective-permute-start(f32[256,512]{1,0:T(8,128)S(1)} %get-tuple-element.23), channel_id=1, source_target_pairs={{1,0},{6,4},{9,8},{14,12},{17,16},{22,20},{25,24},{30,28}} | collective-permute-start | bytes 1572872 | tf_op jit(solution)/shard_map/ppermute | solution.py:428
  55.8 0.7 collective-permute-start.13
  56.5 0.0 collective-permute-done.13
  56.5 0.0 collective-permute-done.12
  56.5 33.7 %collective-permute-done.10 = f32[256,512]{1,0:T(8,128)S(1)} collective-permute-done((f32[256,512]{1,0:T(8,128)S(1)}, f32[256,512]{1,0:T(8,128)S(1)}, u32[]{:S(2)}, u32[]{:S(2)}) %collective-permute-start.10) | collective-permute-done | bytes 524320 | tf_op jit(solution)/shard_map/ppermute | solution.py:428
  90.2 5.6 %collective-permute-done.6 = f32[256,512]{1,0:T(8,128)S(1)} collective-permute-done((f32[256,512]{1,0:T(8,128)S(1)}, f32[256,512]{1,0:T(8,128)S(1)}, u32[]{:S(2)}, u32[]{:S(2)}) %collective-permute-start.6) | collective-permute-done | bytes 524320 | tf_op jit(solution)/shard_map/ppermute | solution.py:428
  95.8 0.0 collective-permute-done.11
  95.8 1.2 %add_bitcast_fusion = f32[1,256,1024]{2,1,0:T(8,128)} fusion(f32[256,256]{1,0:T(8,128)S(1)} %collective-permute-done.13, f32[256,512]{1,0:T(8,128)S(1)} %collective-permute-done.12, f32[256,768]{1,0:T(8,128)S(1)} %collective-permute-done.11, f32[256,512]{1,0:T(8,128)S(1)} %collective-permute-done.10, f32[256,512]{1,0:T(8,128)S(1)} %collective-permute-done.6), kind=kLoop, calls=%fused_computation | loop fusion | flops 1048576 | bytes 3670016 | tf_op jit(solution)/shard_map/broadcast_in_dim | solution.py:458
  (3 shorter events, 0.0 us)
Async XLA Ops:
  2.5 5.3 %copy-start = (f32[2,128,512]{2,1,0:T(8,128)S(1)}, f32[2,128,512]{2,1,0:T(8,128)}, u32[]{:S(2)}) copy-start(f32[2,128,512]{2,1,0:T(8,128)} %refs_0_.1) | copy-start | bytes 1572868
  2.5 15.0 %all-to-all-start = ((f32[8,32,512]{2,1,0:T(8,128)}), f32[8,32,512]{2,1,0:T(8,128)S(1)}, u32[]{:S(2)}, u32[]{:S(2)}) async-start(f32[8,32,512]{2,1,0:T(8,128)} %bitcast.15), calls=%async_computation | async-start | bytes 1048576 | tf_op jit(solution)/shard_map/all_to_all | solution.py:438
  7.8 15.5 %collective-permute-start.1 = (f32[2,128,512]{2,1,0:T(8,128)S(1)}, f32[2,128,512]{2,1,0:T(8,128)S(1)}, u32[]{:S(2)}, u32[]{:S(2)}) collective-permute-start(f32[2,128,512]{2,1,0:T(8,128)S(1)} %copy-done), channel_id=1, source_target_pairs={{2,1},{7,6},{10,9},{15,14},{18,17},{23,22},{26,25},{31,30}} | collective-permute-start | bytes 1572872 | tf_op jit(solution)/shard_map/ppermute | solution.py:422
  8.5 22.3 %collective-permute-start = (f32[2,128,512]{2,1,0:T(8,128)S(1)}, f32[2,128,512]{2,1,0:T(8,128)S(1)}, u32[]{:S(2)}, u32[]{:S(2)}) collective-permute-start(f32[2,128,512]{2,1,0:T(8,128)S(1)} %copy-done), channel_id=1, source_target_pairs={{0,1},{5,6},{8,9},{13,14},{16,17},{21,22},{24,25},{29,30}} | collective-permute-start | bytes 1572872 | tf_op jit(solution)/shard_map/ppermute | solution.py:422
  12.7 18.9 %collective-permute-start.2 = (f32[2,128,512]{2,1,0:T(8,128)S(1)}, f32[2,128,512]{2,1,0:T(8,128)}, u32[]{:S(2)}, u32[]{:S(2)}) collective-permute-start(f32[2,128,512]{2,1,0:T(8,128)S(1)} %copy-done), channel_id=1, source_target_pairs={{3,1},{4,6},{11,9},{12,14},{19,17},{20,22},{27,25},{28,30}} | collective-permute-start | bytes 1572872 | tf_op jit(solution)/shard_map/ppermute | solution.py:422
  17.5 14.7 %copy-start.1 = (s32[2,512]{1,0:T(2,128)S(1)}, s32[2,512]{1,0:T(2,128)}, u32[]{:S(2)}) copy-start(s32[2,512]{1,0:T(2,128)} %refs_4_.1) | copy-start | bytes 12292
  17.5 14.7 %copy-start.2 = (f32[1,1024]{1,0:T(1,128)S(1)}, f32[1,1024]{1,0:T(1,128)}, u32[]{:S(2)}) copy-start(f32[1,1024]{1,0:T(1,128)} %refs_5_.1) | copy-start | bytes 12292
  17.6 13.3 %all-to-all-start.1 = ((f32[8,32,512]{2,1,0:T(8,128)}), f32[8,32,512]{2,1,0:T(8,128)S(1)}, u32[]{:S(2)}, u32[]{:S(2)}) async-start(f32[8,32,512]{2,1,0:T(8,128)} %bitcast.3), calls=%async_computation.1 | async-start | bytes 1048576 | tf_op jit(solution)/shard_map/all_to_all | solution.py:438
  21.2 12.1 %collective-permute-start.5 = (f32[256,512]{1,0:T(8,128)S(1)}, f32[256,512]{1,0:T(8,128)S(1)}, u32[]{:S(2)}, u32[]{:S(2)}) collective-permute-start(f32[256,512]{1,0:T(8,128)S(1)} %bitcast.7), channel_id=1, source_target_pairs={{3,1},{4,6},{11,9},{12,14},{19,17},{20,22},{27,25},{28,30}} | collective-permute-start | bytes 1572872 | tf_op jit(solution)/shard_map/ppermute | solution.py:422
  21.9 23.2 %collective-permute-start.4 = (f32[256,512]{1,0:T(8,128)S(1)}, f32[256,512]{1,0:T(8,128)}, u32[]{:S(2)}, u32[]{:S(2)}) collective-permute-start(f32[256,512]{1,0:T(8,128)S(1)} %bitcast.8), channel_id=1, source_target_pairs={{2,1},{7,6},{10,9},{15,14},{18,17},{23,22},{26,25},{31,30}} | collective-permute-start | bytes 1572872 | tf_op jit(solution)/shard_map/ppermute | solution.py:422
  23.4 21.7 %collective-permute-start.3 = (f32[256,512]{1,0:T(8,128)S(1)}, f32[256,512]{1,0:T(8,128)}, u32[]{:S(2)}, u32[]{:S(2)}) collective-permute-start(f32[256,512]{1,0:T(8,128)S(1)} %bitcast.9), channel_id=1, source_target_pairs={{0,1},{5,6},{8,9},{13,14},{16,17},{21,22},{24,25},{29,30}} | collective-permute-start | bytes 1572872 | tf_op jit(solution)/shard_map/ppermute | solution.py:422
  30.8 15.5 %collective-permute-start.9 = (f32[256,512]{1,0:T(8,128)S(1)}, f32[256,512]{1,0:T(8,128)S(1)}, u32[]{:S(2)}, u32[]{:S(2)}) collective-permute-start(f32[256,512]{1,0:T(8,128)S(1)} %bitcast.11), channel_id=1, source_target_pairs={{3,1},{4,6},{11,9},{12,14},{19,17},{20,22},{27,25},{28,30}} | collective-permute-start | bytes 1572872 | tf_op jit(solution)/shard_map/ppermute | solution.py:422
  31.5 14.8 %collective-permute-start.8 = (f32[256,512]{1,0:T(8,128)S(1)}, f32[256,512]{1,0:T(8,128)S(1)}, u32[]{:S(2)}, u32[]{:S(2)}) collective-permute-start(f32[256,512]{1,0:T(8,128)S(1)} %bitcast.12), channel_id=1, source_target_pairs={{2,1},{7,6},{10,9},{15,14},{18,17},{23,22},{26,25},{31,30}} | collective-permute-start | bytes 1572872 | tf_op jit(solution)/shard_map/ppermute | solution.py:422
  33.3 18.4 %collective-permute-start.7 = (f32[256,512]{1,0:T(8,128)S(1)}, f32[256,512]{1,0:T(8,128)S(1)}, u32[]{:S(2)}, u32[]{:S(2)}) collective-permute-start(f32[256,512]{1,0:T(8,128)S(1)} %bitcast.13), channel_id=1, source_target_pairs={{0,1},{5,6},{8,9},{13,14},{16,17},{21,22},{24,25},{29,30}} | collective-permute-start | bytes 1572872 | tf_op jit(solution)/shard_map/ppermute | solution.py:422
  51.7 44.1 %collective-permute-start.11 = (f32[256,768]{1,0:T(8,128)S(1)}, f32[256,768]{1,0:T(8,128)S(1)}, u32[]{:S(2)}, u32[]{:S(2)}) collective-permute-start(f32[256,768]{1,0:T(8,128)S(1)} %get-tuple-element.32), channel_id=1, source_target_pairs={{1,1},{6,5},{9,9},{14,13},{17,17},{22,21},{25,25},{30,29}} | collective-permute-start | bytes 2359304 | tf_op jit(solution)/shard_map/ppermute | solution.py:428
  52.5 4.0 %collective-permute-start.12 = (f32[256,512]{1,0:T(8,128)S(1)}, f32[256,512]{1,0:T(8,128)S(1)}, u32[]{:S(2)}, u32[]{:S(2)}) collective-permute-start(f32[256,512]{1,0:T(8,128)S(1)} %factor_block.2.refs_1_), channel_id=1, source_target_pairs={{1,2},{6,6},{9,10},{14,14},{17,18},{22,22},{25,26},{30,30}} | collective-permute-start | bytes 1572872 | tf_op jit(solution)/shard_map/ppermute | solution.py:428
  53.2 37.1 %collective-permute-start.10 = (f32[256,512]{1,0:T(8,128)S(1)}, f32[256,512]{1,0:T(8,128)S(1)}, u32[]{:S(2)}, u32[]{:S(2)}) collective-permute-start(f32[256,512]{1,0:T(8,128)S(1)} %get-tuple-element.31), channel_id=1, source_target_pairs={{1,0},{6,4},{9,8},{14,12},{17,16},{22,20},{25,24},{30,28}} | collective-permute-start | bytes 1572872 | tf_op jit(solution)/shard_map/ppermute | solution.py:428
  54.5 41.4 %collective-permute-start.6 = (f32[256,512]{1,0:T(8,128)S(1)}, f32[256,512]{1,0:T(8,128)S(1)}, u32[]{:S(2)}, u32[]{:S(2)}) collective-permute-start(f32[256,512]{1,0:T(8,128)S(1)} %get-tuple-element.23), channel_id=1, source_target_pairs={{1,0},{6,4},{9,8},{14,12},{17,16},{22,20},{25,24},{30,28}} | collective-permute-start | bytes 1572872 | tf_op jit(solution)/shard_map/ppermute | solution.py:428
  55.8 0.7 collective-permute-start.13

commit v2 on v1

--- a/solution.py
+++ b/solution.py
@@ -8,7 +8,6 @@
 from jax.sharding import PartitionSpec as P
 
 
-HIGHEST = lax.Precision.HIGHEST
 TILE = 128
 AXES = ("front", "sub")
 
@@ -28,10 +27,6 @@
     @pl.when(lax.axis_index("sub") == leader_of(lax.axis_index("front"), lax.axis_size("sub")))
     def _():
         body(*refs)
-
-
-def dot(a, b, ca=1, cb=0):
-    return lax.dot_general(a, b, (((ca,), (cb,)), ((), ())), precision=HIGHEST, preferred_element_type=f32)
 
 
 def dot16(a, b, ca, cb):
@@ -130,7 +125,7 @@
             parts += z + [jnp.zeros((n - lo - width, n), f32)]
             zpad = jnp.concatenate(parts, axis=0)
             lane_r = lax.broadcasted_iota(jnp.int32, rest.shape, 1)
-            rest = jnp.where((lane_r >= lo) & (lane_r < lo + width), 0.0, rest) - dot(rest, zpad)
+            rest = jnp.where((lane_r >= lo) & (lane_r < lo + width), 0.0, rest) - dot3(rest, zpad)
             nxt = [rest[8 * v:8 * v + 8, :] for v in range(per)]
             rest = rest[width:, :]
 
@@ -178,10 +173,10 @@
     g_ref = refs[0]
     prev = refs[1:1 + nprev]
     r_ref = refs[1 + nprev]
-    rows = g_ref.shape[0]
+    rows, cols = g_ref.shape
     u = g_ref[...]
     for t in range(nprev):
-        off = rows * (nprev - t)
+        off = prev[t].shape[1] - cols
         u = u - dot3(prev[t][:, off:off + rows], prev[t][:, off:], 0, 0)
     r_ref[...] = u
     factor_loop(*refs[1 + nprev:], width)
@@ -226,20 +221,23 @@
     return total
 
 
-def route_kernel(capacity, rows_ref, row_ref, *out_refs):
+def route_kernel(capacity, rows_ref, row_ref, out_ref):
     n = rows_ref.shape[0]
-    slots, width = out_refs[0].shape
+    slots, width = out_ref.shape
     down = lax.broadcasted_iota(jnp.int32, (n, n), 0)
     across = lax.broadcasted_iota(jnp.int32, (n, n), 1)
     row = row_ref[...].astype(f32)
     column = jnp.sum(jnp.where(down == across, jnp.broadcast_to(row, (n, n)), 0.0), axis=1, keepdims=True)
     earlier = (column == row) & (down < across)
     position = jnp.sum(jnp.where(earlier, 1.0, 0.0), axis=0, keepdims=True)
-    slot = row_ref[...] * capacity + position.astype(jnp.int32)
-    pick = lax.broadcasted_iota(jnp.int32, (slots, n), 0) == slot
-    pick = pick.astype(f32).astype(jnp.bfloat16)
-    for h, out_ref in enumerate(out_refs):
-        out_ref[...] = pick_exact(pick, rows_ref[:, h * width:(h + 1) * width], 1, 0, True)
+    total = None
+    for h in range(2):
+        slot = (2 * row_ref[...] + h) * capacity + position.astype(jnp.int32)
+        pick = lax.broadcasted_iota(jnp.int32, (slots, n), 0) == slot
+        pick = pick.astype(f32).astype(jnp.bfloat16)
+        part = pick_exact(pick, rows_ref[:, h * width:(h + 1) * width], 1, 0, True)
+        total = part if total is None else total + part
+    out_ref[...] = total
 
 
 def route(row_values, front_of_row, fronts):
@@ -247,9 +245,9 @@
     capacity = 2 * n // fronts
     return pl.pallas_call(
         functools.partial(route_kernel, capacity),
-        out_shape=[jax.ShapeDtypeStruct((fronts * capacity, width // 2), f32)] * 2,
+        out_shape=jax.ShapeDtypeStruct((2 * fronts * capacity, width // 2), f32),
         in_specs=[pl.BlockSpec(memory_space=pltpu.VMEM)] * 2,
-        out_specs=[pl.BlockSpec(memory_space=pltpu.VMEM)] * 2,
+        out_specs=pl.BlockSpec(memory_space=pltpu.VMEM),
         cost_estimate=cost(3),
         name="route",
     )(row_values, front_of_row.reshape(1, n))
@@ -388,7 +386,12 @@
         lo = (s - nlead) * block
         left = high1[:, lo:lo + block], low1[:, lo:lo + block]
         done = pair_dot(left, (high1[:, lo:], low1[:, lo:]), 0, 0)
-        outs[s][...] = grams[s][...] + gram_block(high_ref, low_ref, lo, block) - done
+        total = grams[s][...] + gram_block(high_ref, low_ref, lo, block) - done
+        if s < nblocks - 1:
+            outs[s][...] = total
+            continue
+        for q, out_ref in enumerate(outs[s:]):
+            out_ref[...] = total[q * TILE:(q + 1) * TILE, q * TILE:]
 
 
 def cross_update(grams, parts, lead, keep, high1, low1):
@@ -398,6 +401,7 @@
     ins = [*grams, *parts, lead, keep, high1, low1]
     shapes = [jax.ShapeDtypeStruct(g.shape, f32) for g in grams]
     shapes[0] = jax.ShapeDtypeStruct((block, grams[0].shape[1] - cols), f32)
+    shapes[-1:] = [jax.ShapeDtypeStruct((TILE, block - at), f32) for at in range(0, block, TILE)]
     tall = (rows * len(parts), cols)
     return pl.pallas_call(
         functools.partial(on_leader, functools.partial(cross_kernel, len(grams), nlead, len(parts))),
@@ -433,28 +437,34 @@
     width = row_values.shape[1]
     block = width // subs
     kid_parts = to_leader(child_factors, fronts, subs)
+    routed = route(row_values, front_of_row, fronts)
+    received = lax.all_to_all(routed, "front", split_axis=0, concat_axis=0, tiled=True)
+    received = received.reshape(fronts, 2, -1, width // 2)
     halves = []
-    for outgoing in route(row_values, front_of_row, fronts):
-        received = lax.all_to_all(outgoing, "front", split_axis=0, concat_axis=0, tiled=True)
-        halves.append(to_leader(received, fronts, subs))
+    for h in range(2):
+        own = received[:, h].reshape(-1, width // 2)
+        halves.append(to_leader(own, fronts, subs))
     grams = children_gram(kid_parts, child_columns, damping, block)
     lead, top, keep, high1, low1 = lead_factor(grams, halves[0])
     pieces = []
 
-    def send(x, owner, at):
+    def send(x, owner, row, at):
         sent = from_leader(x, owner, fronts, subs)
-        pieces.append(jnp.pad(sent, ((0, 0), (at, width - at - x.shape[1]))))
+        below = block - row - x.shape[0]
+        pieces.append(jnp.pad(sent, ((row, below), (at, width - at - x.shape[1]))))
 
     nlead = subs // 2
-    send(top, 0, 0)
+    send(top, 0, 0, 0)
     rest = cross_update(grams, halves[1], lead, keep, high1, low1)
-    send(rest[0], 0, nlead * block)
+    send(rest[0], 0, 0, nlead * block)
     for s in range(1, nlead):
-        send(rest[s], s, s * block)
+        send(rest[s], s, 0, s * block)
     factors = []
-    for s in range(nlead, subs):
-        factors.append(chol_block(rest[s], factors))
-        send(factors[-1], s, s * block)
+    for n, gram in enumerate(rest[nlead:]):
+        owner = min(nlead + n, subs - 1)
+        at = width - gram.shape[1]
+        factors.append(chol_block(gram, factors))
+        send(factors[-1], owner, at - owner * block, at)
     return functools.reduce(jnp.add, pieces)[None]
 
 

time: 97.6 us -> 95.4 us (0.977)
  starting transfers between devices: 39.9 us -> 31.3 us
  waiting for transfers between devices: 51 us -> 59 us
  Pallas kernels: 4.8 us -> 3.19 us
    ppermute x9, starting transfers between devices: 26.3 us -> 20.7 us  [to_leader(): parts.append(lax.ppermute(x, AXES, pairs))]
    ppermute x9, waiting for transfers between devices: 5.44 us -> 10.8 us  [to_leader(): parts.append(lax.ppermute(x, AXES, pairs))]
    all_to_all x2 -> x1, waiting for transfers between devices: 6.16 us -> 10.5 us  [local(): lax.all_to_all(routed, 'front', split_axis=0, concat_axis=0, tiled=True)]
    all_to_all x2 -> x1, starting transfers between devices: 8.96 us -> 5.33 us  [local(): lax.all_to_all(routed, 'front', split_axis=0, concat_axis=0, tiled=True)]
    ppermute x5 -> x6, waiting for transfers between devices: 39.4 us -> 37.7 us  [from_leader(): return lax.ppermute(x, AXES, pairs)]
    pallas_call x1, Pallas kernels: 1.2 us -> 0.03 us  [lead_factor(): pl.pallas_call(functools.partial(on_leader, functools.partial(lead_kernel...]
    pallas_call x1, Pallas kernels: 1.05 us -> 0.03 us  [children_gram(): pl.pallas_call(functools.partial(on_leader, functools.partial(children_ke...]
    ppermute x5 -> x6, starting transfers between devices: 4.65 us -> 5.31 us  [from_leader(): return lax.ppermute(x, AXES, pairs)]
  transfers between devices with their start and end apart: 16 -> 16, of which waited for: 5 -> 5; matrix products, arithmetic and copies ran while one was open for 0% -> 0% of each run, Pallas kernels for 2% -> 0%
where the time goes in v2:
time: 95.4 us; the launch traced here: 95 us
  waiting for transfers between devices  59 us (62%)
  starting transfers between devices  31.3 us (33%)
  Pallas kernels  3.19 us (3%)
  other arithmetic  1.15 us (1%)
    ppermute x6, waiting for transfers between devices, from_leader(): return lax.ppermute(x, AXES, pairs)  37.7 us
    ppermute x9, starting transfers between devices, to_leader(): parts.append(lax.ppermute(x, AXES, pairs))  20.7 us
    ppermute x9, waiting for transfers between devices, to_leader(): parts.append(lax.ppermute(x, AXES, pairs))  10.8 us
    all_to_all x1, waiting for transfers between devices, local(): lax.all_to_all(routed, 'front', split_axis=0, concat_axis=0, tiled=True)  10.5 us
    all_to_all x1, starting transfers between devices, local(): lax.all_to_all(routed, 'front', split_axis=0, concat_axis=0, tiled=True)  5.33 us
    ppermute x6, starting transfers between devices, from_leader(): return lax.ppermute(x, AXES, pairs)  5.31 us
    pallas_call x1, Pallas kernels, route(): pl.pallas_call(functools.partial(route_kernel, capacity), out_shape=jax.S...  3.07 us
  transfers between devices with their start and end apart: 16, of which 5 were waited for; matrix products, arithmetic and copies ran while one was open for 0% of the time, Pallas kernels for 0%

profile of v2, /device:TPU:0, one launch (start us, length us, event | category | flops | bytes accessed | tf_op | source)
XLA Modules:
  0.0 95.0 jit_solution(1512623463229852065)
XLA Ops:
  0.0 3.1 %route.1 = f32[512,512]{1,0:T(8,128)} custom-call(f32[128,1024]{1,0:T(8,128)} %rows_ref.1, s32[1,128]{1,0:T(1,128)} %bitcast.17), custom_call_target="tpu_custom_call" | custom-call | flops 1500000000 | tf_op jit(solution)/shard_map/route/pallas_call | solution.py:246
  3.1 0.0 copy-start
  3.1 5.3 %all-to-all-start = ((f32[8,64,512]{2,1,0:T(8,128)}), f32[8,64,512]{2,1,0:T(8,128)S(1)}, u32[]{:S(2)}, u32[]{:S(2)}) async-start(f32[8,64,512]{2,1,0:T(8,128)} %bitcast.16), calls=%async_computation | async-start | bytes 2097152 | tf_op jit(solution)/shard_map/all_to_all | solution.py:441
  8.4 0.0 copy-done
  8.4 3.5 %collective-permute-start = (f32[2,128,512]{2,1,0:T(8,128)S(1)}, f32[2,128,512]{2,1,0:T(8,128)S(1)}, u32[]{:S(2)}, u32[]{:S(2)}) collective-permute-start(f32[2,128,512]{2,1,0:T(8,128)S(1)} %copy-done), channel_id=1, source_target_pairs={{0,1},{5,6},{8,9},{13,14},{16,17},{21,22},{24,25},{29,30}} | collective-permute-start | bytes 1572872 | tf_op jit(solution)/shard_map/ppermute | solution.py:426
  11.9 0.7 collective-permute-start.1
  12.6 0.7 collective-permute-start.2
  13.3 10.5 %all-to-all-done = f32[8,64,512]{2,1,0:T(8,128)S(1)} async-done(((f32[8,64,512]{2,1,0:T(8,128)}), f32[8,64,512]{2,1,0:T(8,128)S(1)}, u32[]{:S(2)}, u32[]{:S(2)}) %all-to-all-start) | async-done | bytes 1048608 | tf_op jit(solution)/shard_map/all_to_all | solution.py:441
  23.8 0.0 copy-start.1
  23.8 0.0 copy-start.2
  23.8 0.1 fusion
  23.9 3.5 %collective-permute-start.3 = (f32[256,512]{1,0:T(8,128)S(1)}, f32[256,512]{1,0:T(8,128)S(1)}, u32[]{:S(2)}, u32[]{:S(2)}) collective-permute-start(f32[256,512]{1,0:T(8,128)S(1)} %bitcast.11), channel_id=1, source_target_pairs={{0,1},{5,6},{8,9},{13,14},{16,17},{21,22},{24,25},{29,30}} | collective-permute-start | bytes 1572872 | tf_op jit(solution)/shard_map/ppermute | solution.py:426
  27.4 0.7 collective-permute-start.4
  28.1 0.0 collective-permute-done.refs_1_
  28.1 0.7 collective-permute-start.5
  28.8 0.0 collective-permute-done.1.refs_2_
  28.8 0.0 collective-permute-done.2.refs_3_
  28.8 0.0 copy-done.1
  28.8 0.0 copy-done.2
  28.9 9.5 %collective-permute-start.7 = (f32[256,512]{1,0:T(8,128)S(1)}, f32[256,512]{1,0:T(8,128)S(1)}, u32[]{:S(2)}, u32[]{:S(2)}) collective-permute-start(f32[256,512]{1,0:T(8,128)S(1)} %bitcast.7), channel_id=1, source_target_pairs={{0,1},{5,6},{8,9},{13,14},{16,17},{21,22},{24,25},{29,30}} | collective-permute-start | bytes 1572872 | tf_op jit(solution)/shard_map/ppermute | solution.py:426
  38.4 0.7 collective-permute-start.8
  39.1 0.5 collective-permute-done.3.refs_3_
  39.6 0.7 collective-permute-start.9
  40.3 0.0 collective-permute-done.4.refs_4_
  40.3 0.0 collective-permute-done.5.refs_5_
  40.4 10.3 %collective-permute-done.7.refs_5_ = f32[256,512]{1,0:T(8,128)S(1)} collective-permute-done((f32[256,512]{1,0:T(8,128)S(1)}, f32[256,512]{1,0:T(8,128)S(1)}, u32[]{:S(2)}, u32[]{:S(2)}) %collective-permute-start.7) | collective-permute-done | bytes 524320 | tf_op jit(solution)/shard_map/ppermute | solution.py:426
  50.6 0.0 collective-permute-done.8.refs_6_
  50.6 0.0 collective-permute-done.9.refs_7_
  50.7 0.7 collective-permute-start.11
  51.4 0.7 collective-permute-start.12
  52.1 1.3 %collective-permute-start.10 = (f32[256,512]{1,0:T(8,128)S(1)}, f32[256,512]{1,0:T(8,128)S(1)}, u32[]{:S(2)}, u32[]{:S(2)}) collective-permute-start(f32[256,512]{1,0:T(8,128)S(1)} %get-tuple-element.28), channel_id=1, source_target_pairs={{1,0},{6,4},{9,8},{14,12},{17,16},{22,20},{25,24},{30,28}} | collective-permute-start | bytes 1572872 | tf_op jit(solution)/shard_map/ppermute | solution.py:432
  53.4 1.3 %collective-permute-start.6 = (f32[256,512]{1,0:T(8,128)S(1)}, f32[256,512]{1,0:T(8,128)S(1)}, u32[]{:S(2)}, u32[]{:S(2)}) collective-permute-start(f32[256,512]{1,0:T(8,128)S(1)} %get-tuple-element.21), channel_id=1, source_target_pairs={{1,0},{6,4},{9,8},{14,12},{17,16},{22,20},{25,24},{30,28}} | collective-permute-start | bytes 1572872 | tf_op jit(solution)/shard_map/ppermute | solution.py:432
  54.8 0.7 collective-permute-start.14
  55.4 0.0 collective-permute-done.14
  55.4 0.7 collective-permute-start.13
  56.1 0.0 collective-permute-done.13
  56.1 0.0 collective-permute-done.12
  56.1 32.1 %collective-permute-done.10 = f32[256,512]{1,0:T(8,128)S(1)} collective-permute-done((f32[256,512]{1,0:T(8,128)S(1)}, f32[256,512]{1,0:T(8,128)S(1)}, u32[]{:S(2)}, u32[]{:S(2)}) %collective-permute-start.10) | collective-permute-done | bytes 524320 | tf_op jit(solution)/shard_map/ppermute | solution.py:432
  88.2 5.6 %collective-permute-done.6 = f32[256,512]{1,0:T(8,128)S(1)} collective-permute-done((f32[256,512]{1,0:T(8,128)S(1)}, f32[256,512]{1,0:T(8,128)S(1)}, u32[]{:S(2)}, u32[]{:S(2)}) %collective-permute-start.6) | collective-permute-done | bytes 524320 | tf_op jit(solution)/shard_map/ppermute | solution.py:432
  93.8 0.0 collective-permute-done.11
  93.8 1.1 %add_bitcast_fusion = f32[1,256,1024]{2,1,0:T(8,128)} fusion(f32[128,128]{1,0:T(8,128)S(1)} %collective-permute-done.14, f32[128,256]{1,0:T(8,128)S(1)} %collective-permute-done.13, f32[256,512]{1,0:T(8,128)S(1)} %collective-permute-done.12, f32[256,768]{1,0:T(8,128)S(1)} %collective-permute-done.11, f32[256,512]{1,0:T(8,128)S(1)} %collective-permute-done.10, ...), kind=kLoop, calls=%fused_computation | loop fusion | flops 1310720 | bytes 3604480 | tf_op jit(solution)/shard_map/broadcast_in_dim | solution.py:468
  (6 shorter events, 0.1 us)
Async XLA Ops:
  3.1 5.3 %copy-start = (f32[2,128,512]{2,1,0:T(8,128)S(1)}, f32[2,128,512]{2,1,0:T(8,128)}, u32[]{:S(2)}) copy-start(f32[2,128,512]{2,1,0:T(8,128)} %refs_0_.1) | copy-start | bytes 1572868
  3.1 20.7 %all-to-all-start = ((f32[8,64,512]{2,1,0:T(8,128)}), f32[8,64,512]{2,1,0:T(8,128)S(1)}, u32[]{:S(2)}, u32[]{:S(2)}) async-start(f32[8,64,512]{2,1,0:T(8,128)} %bitcast.16), calls=%async_computation | async-start | bytes 2097152 | tf_op jit(solution)/shard_map/all_to_all | solution.py:441
  8.4 19.7 %collective-permute-start = (f32[2,128,512]{2,1,0:T(8,128)S(1)}, f32[2,128,512]{2,1,0:T(8,128)S(1)}, u32[]{:S(2)}, u32[]{:S(2)}) collective-permute-start(f32[2,128,512]{2,1,0:T(8,128)S(1)} %copy-done), channel_id=1, source_target_pairs={{0,1},{5,6},{8,9},{13,14},{16,17},{21,22},{24,25},{29,30}} | collective-permute-start | bytes 1572872 | tf_op jit(solution)/shard_map/ppermute | solution.py:426
  11.9 16.9 %collective-permute-start.1 = (f32[2,128,512]{2,1,0:T(8,128)S(1)}, f32[2,128,512]{2,1,0:T(8,128)S(1)}, u32[]{:S(2)}, u32[]{:S(2)}) collective-permute-start(f32[2,128,512]{2,1,0:T(8,128)S(1)} %copy-done), channel_id=1, source_target_pairs={{2,1},{7,6},{10,9},{15,14},{18,17},{23,22},{26,25},{31,30}} | collective-permute-start | bytes 1572872 | tf_op jit(solution)/shard_map/ppermute | solution.py:426
  12.6 16.2 %collective-permute-start.2 = (f32[2,128,512]{2,1,0:T(8,128)S(1)}, f32[2,128,512]{2,1,0:T(8,128)S(1)}, u32[]{:S(2)}, u32[]{:S(2)}) collective-permute-start(f32[2,128,512]{2,1,0:T(8,128)S(1)} %copy-done), channel_id=1, source_target_pairs={{3,1},{4,6},{11,9},{12,14},{19,17},{20,22},{27,25},{28,30}} | collective-permute-start | bytes 1572872 | tf_op jit(solution)/shard_map/ppermute | solution.py:426
  23.8 5.1 %copy-start.1 = (s32[2,512]{1,0:T(2,128)S(1)}, s32[2,512]{1,0:T(2,128)}, u32[]{:S(2)}) copy-start(s32[2,512]{1,0:T(2,128)} %refs_4_.1) | copy-start | bytes 12292
  23.8 5.1 %copy-start.2 = (f32[1,1024]{1,0:T(1,128)S(1)}, f32[1,1024]{1,0:T(1,128)}, u32[]{:S(2)}) copy-start(f32[1,1024]{1,0:T(1,128)} %refs_5_.1) | copy-start | bytes 12292
  23.9 15.7 %collective-permute-start.3 = (f32[256,512]{1,0:T(8,128)S(1)}, f32[256,512]{1,0:T(8,128)S(1)}, u32[]{:S(2)}, u32[]{:S(2)}) collective-permute-start(f32[256,512]{1,0:T(8,128)S(1)} %bitcast.11), channel_id=1, source_target_pairs={{0,1},{5,6},{8,9},{13,14},{16,17},{21,22},{24,25},{29,30}} | collective-permute-start | bytes 1572872 | tf_op jit(solution)/shard_map/ppermute | solution.py:426
  27.4 12.9 %collective-permute-start.4 = (f32[256,512]{1,0:T(8,128)S(1)}, f32[256,512]{1,0:T(8,128)S(1)}, u32[]{:S(2)}, u32[]{:S(2)}) collective-permute-start(f32[256,512]{1,0:T(8,128)S(1)} %bitcast.12), channel_id=1, source_target_pairs={{2,1},{7,6},{10,9},{15,14},{18,17},{23,22},{26,25},{31,30}} | collective-permute-start | bytes 1572872 | tf_op jit(solution)/shard_map/ppermute | solution.py:426
  28.1 12.2 %collective-permute-start.5 = (f32[256,512]{1,0:T(8,128)S(1)}, f32[256,512]{1,0:T(8,128)S(1)}, u32[]{:S(2)}, u32[]{:S(2)}) collective-permute-start(f32[256,512]{1,0:T(8,128)S(1)} %bitcast.13), channel_id=1, source_target_pairs={{3,1},{4,6},{11,9},{12,14},{19,17},{20,22},{27,25},{28,30}} | collective-permute-start | bytes 1572872 | tf_op jit(solution)/shard_map/ppermute | solution.py:426
  28.9 21.8 %collective-permute-start.7 = (f32[256,512]{1,0:T(8,128)S(1)}, f32[256,512]{1,0:T(8,128)S(1)}, u32[]{:S(2)}, u32[]{:S(2)}) collective-permute-start(f32[256,512]{1,0:T(8,128)S(1)} %bitcast.7), channel_id=1, source_target_pairs={{0,1},{5,6},{8,9},{13,14},{16,17},{21,22},{24,25},{29,30}} | collective-permute-start | bytes 1572872 | tf_op jit(solution)/shard_map/ppermute | solution.py:426
  38.4 12.2 %collective-permute-start.8 = (f32[256,512]{1,0:T(8,128)S(1)}, f32[256,512]{1,0:T(8,128)S(1)}, u32[]{:S(2)}, u32[]{:S(2)}) collective-permute-start(f32[256,512]{1,0:T(8,128)S(1)} %bitcast.8), channel_id=1, source_target_pairs={{2,1},{7,6},{10,9},{15,14},{18,17},{23,22},{26,25},{31,30}} | collective-permute-start | bytes 1572872 | tf_op jit(solution)/shard_map/ppermute | solution.py:426
  39.6 11.0 %collective-permute-start.9 = (f32[256,512]{1,0:T(8,128)S(1)}, f32[256,512]{1,0:T(8,128)S(1)}, u32[]{:S(2)}, u32[]{:S(2)}) collective-permute-start(f32[256,512]{1,0:T(8,128)S(1)} %bitcast.9), channel_id=1, source_target_pairs={{3,1},{4,6},{11,9},{12,14},{19,17},{20,22},{27,25},{28,30}} | collective-permute-start | bytes 1572872 | tf_op jit(solution)/shard_map/ppermute | solution.py:426
  50.7 43.2 %collective-permute-start.11 = (f32[256,768]{1,0:T(8,128)S(1)}, f32[256,768]{1,0:T(8,128)S(1)}, u32[]{:S(2)}, u32[]{:S(2)}) collective-permute-start(f32[256,768]{1,0:T(8,128)S(1)} %get-tuple-element.29), channel_id=1, source_target_pairs={{1,1},{6,5},{9,9},{14,13},{17,17},{22,21},{25,25},{30,29}} | collective-permute-start | bytes 2359304 | tf_op jit(solution)/shard_map/ppermute | solution.py:432
  51.4 4.7 %collective-permute-start.12 = (f32[256,512]{1,0:T(8,128)S(1)}, f32[256,512]{1,0:T(8,128)S(1)}, u32[]{:S(2)}, u32[]{:S(2)}) collective-permute-start(f32[256,512]{1,0:T(8,128)S(1)} %factor_block.3.refs_1_), channel_id=1, source_target_pairs={{1,2},{6,6},{9,10},{14,14},{17,18},{22,22},{25,26},{30,30}} | collective-permute-start | bytes 1572872 | tf_op jit(solution)/shard_map/ppermute | solution.py:432
  52.1 36.1 %collective-permute-start.10 = (f32[256,512]{1,0:T(8,128)S(1)}, f32[256,512]{1,0:T(8,128)S(1)}, u32[]{:S(2)}, u32[]{:S(2)}) collective-permute-start(f32[256,512]{1,0:T(8,128)S(1)} %get-tuple-element.28), channel_id=1, source_target_pairs={{1,0},{6,4},{9,8},{14,12},{17,16},{22,20},{25,24},{30,28}} | collective-permute-start | bytes 1572872 | tf_op jit(solution)/shard_map/ppermute | solution.py:432
  53.4 40.4 %collective-permute-start.6 = (f32[256,512]{1,0:T(8,128)S(1)}, f32[256,512]{1,0:T(8,128)S(1)}, u32[]{:S(2)}, u32[]{:S(2)}) collective-permute-start(f32[256,512]{1,0:T(8,128)S(1)} %get-tuple-element.21), channel_id=1, source_target_pairs={{1,0},{6,4},{9,8},{14,12},{17,16},{22,20},{25,24},{30,28}} | collective-permute-start | bytes 1572872 | tf_op jit(solution)/shard_map/ppermute | solution.py:432
  54.8 0.7 collective-permute-start.14
  55.4 0.7 collective-permute-start.13

commit v3 on v2

--- a/solution.py
+++ b/solution.py
@@ -230,9 +230,20 @@
     column = jnp.sum(jnp.where(down == across, jnp.broadcast_to(row, (n, n)), 0.0), axis=1, keepdims=True)
     earlier = (column == row) & (down < across)
     position = jnp.sum(jnp.where(earlier, 1.0, 0.0), axis=0, keepdims=True)
+    position = position.astype(jnp.int32)
+    if capacity % 8 == 0:
+        half = slots // 2
+        pick = lax.broadcasted_iota(jnp.int32, (half, n), 0) == row_ref[...] * capacity + position
+        pick = pick.astype(f32).astype(jnp.bfloat16)
+        for h in range(2):
+            part = pick_exact(pick, rows_ref[:, h * width:(h + 1) * width], 1, 0, True)
+            for at in range(0, half, capacity):
+                to = 2 * at + h * capacity
+                out_ref[to:to + capacity, :] = part[at:at + capacity, :]
+        return
     total = None
     for h in range(2):
-        slot = (2 * row_ref[...] + h) * capacity + position.astype(jnp.int32)
+        slot = (2 * row_ref[...] + h) * capacity + position
         pick = lax.broadcasted_iota(jnp.int32, (slots, n), 0) == slot
         pick = pick.astype(f32).astype(jnp.bfloat16)
         part = pick_exact(pick, rows_ref[:, h * width:(h + 1) * width], 1, 0, True)

time: 95.4 us -> 95 us (level)
  no operation moved by 1% of the time
where the time goes in v3:
time: 95 us; the launch traced here: 94.6 us
  waiting for transfers between devices  58.9 us (62%)
  starting transfers between devices  31.3 us (33%)
  Pallas kernels  2.78 us (3%)
  other arithmetic  1.15 us (1%)
    ppermute x6, waiting for transfers between devices, from_leader(): return lax.ppermute(x, AXES, pairs)  37.7 us
    ppermute x9, starting transfers between devices, to_leader(): parts.append(lax.ppermute(x, AXES, pairs))  20.7 us
    ppermute x9, waiting for transfers between devices, to_leader(): parts.append(lax.ppermute(x, AXES, pairs))  10.8 us
    all_to_all x1, waiting for transfers between devices, local(): lax.all_to_all(routed, 'front', split_axis=0, concat_axis=0, tiled=True)  10.4 us
    all_to_all x1, starting transfers between devices, local(): lax.all_to_all(routed, 'front', split_axis=0, concat_axis=0, tiled=True)  5.34 us
    ppermute x6, starting transfers between devices, from_leader(): return lax.ppermute(x, AXES, pairs)  5.31 us
    pallas_call x1, Pallas kernels, route(): pl.pallas_call(functools.partial(route_kernel, capacity), out_shape=jax.S...  2.66 us
  transfers between devices with their start and end apart: 16, of which 5 were waited for; matrix products, arithmetic and copies ran while one was open for 0% of the time, Pallas kernels for 0%

profile of v3, /device:TPU:0, one launch (start us, length us, event | category | flops | bytes accessed | tf_op | source)
XLA Modules:
  0.0 94.6 jit_solution(4345936659202965268)
XLA Ops:
  0.0 2.7 %route.1 = f32[512,512]{1,0:T(8,128)} custom-call(f32[128,1024]{1,0:T(8,128)} %rows_ref.1, s32[1,128]{1,0:T(1,128)} %bitcast.17), custom_call_target="tpu_custom_call" | custom-call | flops 1500000000 | tf_op jit(solution)/shard_map/route/pallas_call | solution.py:257
  2.7 0.0 copy-start
  2.7 5.3 %all-to-all-start = ((f32[8,64,512]{2,1,0:T(8,128)}), f32[8,64,512]{2,1,0:T(8,128)S(1)}, u32[]{:S(2)}, u32[]{:S(2)}) async-start(f32[8,64,512]{2,1,0:T(8,128)} %bitcast.16), calls=%async_computation | async-start | bytes 2097152 | tf_op jit(solution)/shard_map/all_to_all | solution.py:452
  8.0 0.0 copy-done
  8.0 3.5 %collective-permute-start = (f32[2,128,512]{2,1,0:T(8,128)S(1)}, f32[2,128,512]{2,1,0:T(8,128)S(1)}, u32[]{:S(2)}, u32[]{:S(2)}) collective-permute-start(f32[2,128,512]{2,1,0:T(8,128)S(1)} %copy-done), channel_id=1, source_target_pairs={{0,1},{5,6},{8,9},{13,14},{16,17},{21,22},{24,25},{29,30}} | collective-permute-start | bytes 1572872 | tf_op jit(solution)/shard_map/ppermute | solution.py:437
  11.5 0.7 collective-permute-start.1
  12.2 0.7 collective-permute-start.2
  12.9 10.4 %all-to-all-done = f32[8,64,512]{2,1,0:T(8,128)S(1)} async-done(((f32[8,64,512]{2,1,0:T(8,128)}), f32[8,64,512]{2,1,0:T(8,128)S(1)}, u32[]{:S(2)}, u32[]{:S(2)}) %all-to-all-start) | async-done | bytes 1048608 | tf_op jit(solution)/shard_map/all_to_all | solution.py:452
  23.4 0.0 copy-start.1
  23.4 0.0 copy-start.2
  23.4 0.1 fusion
  23.5 3.5 %collective-permute-start.3 = (f32[256,512]{1,0:T(8,128)S(1)}, f32[256,512]{1,0:T(8,128)S(1)}, u32[]{:S(2)}, u32[]{:S(2)}) collective-permute-start(f32[256,512]{1,0:T(8,128)S(1)} %bitcast.11), channel_id=1, source_target_pairs={{0,1},{5,6},{8,9},{13,14},{16,17},{21,22},{24,25},{29,30}} | collective-permute-start | bytes 1572872 | tf_op jit(solution)/shard_map/ppermute | solution.py:437
  27.0 0.7 collective-permute-start.4
  27.7 0.0 collective-permute-done.refs_1_
  27.7 0.7 collective-permute-start.5
  28.4 0.0 collective-permute-done.1.refs_2_
  28.4 0.0 collective-permute-done.2.refs_3_
  28.4 0.0 copy-done.1
  28.4 0.0 copy-done.2
  28.5 9.5 %collective-permute-start.7 = (f32[256,512]{1,0:T(8,128)S(1)}, f32[256,512]{1,0:T(8,128)S(1)}, u32[]{:S(2)}, u32[]{:S(2)}) collective-permute-start(f32[256,512]{1,0:T(8,128)S(1)} %bitcast.7), channel_id=1, source_target_pairs={{0,1},{5,6},{8,9},{13,14},{16,17},{21,22},{24,25},{29,30}} | collective-permute-start | bytes 1572872 | tf_op jit(solution)/shard_map/ppermute | solution.py:437
  38.0 0.7 collective-permute-start.8
  38.7 0.5 collective-permute-done.3.refs_3_
  39.2 0.7 collective-permute-start.9
  39.9 0.0 collective-permute-done.4.refs_4_
  39.9 0.0 collective-permute-done.5.refs_5_
  40.0 10.3 %collective-permute-done.7.refs_5_ = f32[256,512]{1,0:T(8,128)S(1)} collective-permute-done((f32[256,512]{1,0:T(8,128)S(1)}, f32[256,512]{1,0:T(8,128)S(1)}, u32[]{:S(2)}, u32[]{:S(2)}) %collective-permute-start.7) | collective-permute-done | bytes 524320 | tf_op jit(solution)/shard_map/ppermute | solution.py:437
  50.2 0.0 collective-permute-done.8.refs_6_
  50.2 0.0 collective-permute-done.9.refs_7_
  50.2 0.7 collective-permute-start.11
  51.0 0.7 collective-permute-start.12
  51.7 1.3 %collective-permute-start.10 = (f32[256,512]{1,0:T(8,128)S(1)}, f32[256,512]{1,0:T(8,128)S(1)}, u32[]{:S(2)}, u32[]{:S(2)}) collective-permute-start(f32[256,512]{1,0:T(8,128)S(1)} %get-tuple-element.28), channel_id=1, source_target_pairs={{1,0},{6,4},{9,8},{14,12},{17,16},{22,20},{25,24},{30,28}} | collective-permute-start | bytes 1572872 | tf_op jit(solution)/shard_map/ppermute | solution.py:443
  53.0 1.3 %collective-permute-start.6 = (f32[256,512]{1,0:T(8,128)S(1)}, f32[256,512]{1,0:T(8,128)S(1)}, u32[]{:S(2)}, u32[]{:S(2)}) collective-permute-start(f32[256,512]{1,0:T(8,128)S(1)} %get-tuple-element.21), channel_id=1, source_target_pairs={{1,0},{6,4},{9,8},{14,12},{17,16},{22,20},{25,24},{30,28}} | collective-permute-start | bytes 1572872 | tf_op jit(solution)/shard_map/ppermute | solution.py:443
  54.3 0.7 collective-permute-start.14
  55.0 0.0 collective-permute-done.14
  55.0 0.7 collective-permute-start.13
  55.7 0.0 collective-permute-done.13
  55.7 0.0 collective-permute-done.12
  55.7 32.1 %collective-permute-done.10 = f32[256,512]{1,0:T(8,128)S(1)} collective-permute-done((f32[256,512]{1,0:T(8,128)S(1)}, f32[256,512]{1,0:T(8,128)S(1)}, u32[]{:S(2)}, u32[]{:S(2)}) %collective-permute-start.10) | collective-permute-done | bytes 524320 | tf_op jit(solution)/shard_map/ppermute | solution.py:443
  87.8 5.6 %collective-permute-done.6 = f32[256,512]{1,0:T(8,128)S(1)} collective-permute-done((f32[256,512]{1,0:T(8,128)S(1)}, f32[256,512]{1,0:T(8,128)S(1)}, u32[]{:S(2)}, u32[]{:S(2)}) %collective-permute-start.6) | collective-permute-done | bytes 524320 | tf_op jit(solution)/shard_map/ppermute | solution.py:443
  93.4 0.0 collective-permute-done.11
  93.4 1.1 %add_bitcast_fusion = f32[1,256,1024]{2,1,0:T(8,128)} fusion(f32[128,128]{1,0:T(8,128)S(1)} %collective-permute-done.14, f32[128,256]{1,0:T(8,128)S(1)} %collective-permute-done.13, f32[256,512]{1,0:T(8,128)S(1)} %collective-permute-done.12, f32[256,768]{1,0:T(8,128)S(1)} %collective-permute-done.11, f32[256,512]{1,0:T(8,128)S(1)} %collective-permute-done.10, ...), kind=kLoop, calls=%fused_computation | loop fusion | flops 1310720 | bytes 3604480 | tf_op jit(solution)/shard_map/broadcast_in_dim | solution.py:479
  (6 shorter events, 0.1 us)
Async XLA Ops:
  2.7 5.3 %copy-start = (f32[2,128,512]{2,1,0:T(8,128)S(1)}, f32[2,128,512]{2,1,0:T(8,128)}, u32[]{:S(2)}) copy-start(f32[2,128,512]{2,1,0:T(8,128)} %refs_0_.1) | copy-start | bytes 1572868
  2.7 20.7 %all-to-all-start = ((f32[8,64,512]{2,1,0:T(8,128)}), f32[8,64,512]{2,1,0:T(8,128)S(1)}, u32[]{:S(2)}, u32[]{:S(2)}) async-start(f32[8,64,512]{2,1,0:T(8,128)} %bitcast.16), calls=%async_computation | async-start | bytes 2097152 | tf_op jit(solution)/shard_map/all_to_all | solution.py:452
  8.0 19.7 %collective-permute-start = (f32[2,128,512]{2,1,0:T(8,128)S(1)}, f32[2,128,512]{2,1,0:T(8,128)S(1)}, u32[]{:S(2)}, u32[]{:S(2)}) collective-permute-start(f32[2,128,512]{2,1,0:T(8,128)S(1)} %copy-done), channel_id=1, source_target_pairs={{0,1},{5,6},{8,9},{13,14},{16,17},{21,22},{24,25},{29,30}} | collective-permute-start | bytes 1572872 | tf_op jit(solution)/shard_map/ppermute | solution.py:437
  11.5 16.9 %collective-permute-start.1 = (f32[2,128,512]{2,1,0:T(8,128)S(1)}, f32[2,128,512]{2,1,0:T(8,128)S(1)}, u32[]{:S(2)}, u32[]{:S(2)}) collective-permute-start(f32[2,128,512]{2,1,0:T(8,128)S(1)} %copy-done), channel_id=1, source_target_pairs={{2,1},{7,6},{10,9},{15,14},{18,17},{23,22},{26,25},{31,30}} | collective-permute-start | bytes 1572872 | tf_op jit(solution)/shard_map/ppermute | solution.py:437
  12.2 16.2 %collective-permute-start.2 = (f32[2,128,512]{2,1,0:T(8,128)S(1)}, f32[2,128,512]{2,1,0:T(8,128)S(1)}, u32[]{:S(2)}, u32[]{:S(2)}) collective-permute-start(f32[2,128,512]{2,1,0:T(8,128)S(1)} %copy-done), channel_id=1, source_target_pairs={{3,1},{4,6},{11,9},{12,14},{19,17},{20,22},{27,25},{28,30}} | collective-permute-start | bytes 1572872 | tf_op jit(solution)/shard_map/ppermute | solution.py:437
  23.4 5.1 %copy-start.1 = (s32[2,512]{1,0:T(2,128)S(1)}, s32[2,512]{1,0:T(2,128)}, u32[]{:S(2)}) copy-start(s32[2,512]{1,0:T(2,128)} %refs_4_.1) | copy-start | bytes 12292
  23.4 5.1 %copy-start.2 = (f32[1,1024]{1,0:T(1,128)S(1)}, f32[1,1024]{1,0:T(1,128)}, u32[]{:S(2)}) copy-start(f32[1,1024]{1,0:T(1,128)} %refs_5_.1) | copy-start | bytes 12292
  23.5 15.7 %collective-permute-start.3 = (f32[256,512]{1,0:T(8,128)S(1)}, f32[256,512]{1,0:T(8,128)S(1)}, u32[]{:S(2)}, u32[]{:S(2)}) collective-permute-start(f32[256,512]{1,0:T(8,128)S(1)} %bitcast.11), channel_id=1, source_target_pairs={{0,1},{5,6},{8,9},{13,14},{16,17},{21,22},{24,25},{29,30}} | collective-permute-start | bytes 1572872 | tf_op jit(solution)/shard_map/ppermute | solution.py:437
  27.0 12.9 %collective-permute-start.4 = (f32[256,512]{1,0:T(8,128)S(1)}, f32[256,512]{1,0:T(8,128)S(1)}, u32[]{:S(2)}, u32[]{:S(2)}) collective-permute-start(f32[256,512]{1,0:T(8,128)S(1)} %bitcast.12), channel_id=1, source_target_pairs={{2,1},{7,6},{10,9},{15,14},{18,17},{23,22},{26,25},{31,30}} | collective-permute-start | bytes 1572872 | tf_op jit(solution)/shard_map/ppermute | solution.py:437
  27.7 12.2 %collective-permute-start.5 = (f32[256,512]{1,0:T(8,128)S(1)}, f32[256,512]{1,0:T(8,128)S(1)}, u32[]{:S(2)}, u32[]{:S(2)}) collective-permute-start(f32[256,512]{1,0:T(8,128)S(1)} %bitcast.13), channel_id=1, source_target_pairs={{3,1},{4,6},{11,9},{12,14},{19,17},{20,22},{27,25},{28,30}} | collective-permute-start | bytes 1572872 | tf_op jit(solution)/shard_map/ppermute | solution.py:437
  28.5 21.7 %collective-permute-start.7 = (f32[256,512]{1,0:T(8,128)S(1)}, f32[256,512]{1,0:T(8,128)S(1)}, u32[]{:S(2)}, u32[]{:S(2)}) collective-permute-start(f32[256,512]{1,0:T(8,128)S(1)} %bitcast.7), channel_id=1, source_target_pairs={{0,1},{5,6},{8,9},{13,14},{16,17},{21,22},{24,25},{29,30}} | collective-permute-start | bytes 1572872 | tf_op jit(solution)/shard_map/ppermute | solution.py:437
  38.0 12.2 %collective-permute-start.8 = (f32[256,512]{1,0:T(8,128)S(1)}, f32[256,512]{1,0:T(8,128)S(1)}, u32[]{:S(2)}, u32[]{:S(2)}) collective-permute-start(f32[256,512]{1,0:T(8,128)S(1)} %bitcast.8), channel_id=1, source_target_pairs={{2,1},{7,6},{10,9},{15,14},{18,17},{23,22},{26,25},{31,30}} | collective-permute-start | bytes 1572872 | tf_op jit(solution)/shard_map/ppermute | solution.py:437
  39.2 11.0 %collective-permute-start.9 = (f32[256,512]{1,0:T(8,128)S(1)}, f32[256,512]{1,0:T(8,128)S(1)}, u32[]{:S(2)}, u32[]{:S(2)}) collective-permute-start(f32[256,512]{1,0:T(8,128)S(1)} %bitcast.9), channel_id=1, source_target_pairs={{3,1},{4,6},{11,9},{12,14},{19,17},{20,22},{27,25},{28,30}} | collective-permute-start | bytes 1572872 | tf_op jit(solution)/shard_map/ppermute | solution.py:437
  50.2 43.2 %collective-permute-start.11 = (f32[256,768]{1,0:T(8,128)S(1)}, f32[256,768]{1,0:T(8,128)S(1)}, u32[]{:S(2)}, u32[]{:S(2)}) collective-permute-start(f32[256,768]{1,0:T(8,128)S(1)} %get-tuple-element.29), channel_id=1, source_target_pairs={{1,1},{6,5},{9,9},{14,13},{17,17},{22,21},{25,25},{30,29}} | collective-permute-start | bytes 2359304 | tf_op jit(solution)/shard_map/ppermute | solution.py:443
  51.0 4.7 %collective-permute-start.12 = (f32[256,512]{1,0:T(8,128)S(1)}, f32[256,512]{1,0:T(8,128)S(1)}, u32[]{:S(2)}, u32[]{:S(2)}) collective-permute-start(f32[256,512]{1,0:T(8,128)S(1)} %factor_block.3.refs_1_), channel_id=1, source_target_pairs={{1,2},{6,6},{9,10},{14,14},{17,18},{22,22},{25,26},{30,30}} | collective-permute-start | bytes 1572872 | tf_op jit(solution)/shard_map/ppermute | solution.py:443
  51.7 36.1 %collective-permute-start.10 = (f32[256,512]{1,0:T(8,128)S(1)}, f32[256,512]{1,0:T(8,128)S(1)}, u32[]{:S(2)}, u32[]{:S(2)}) collective-permute-start(f32[256,512]{1,0:T(8,128)S(1)} %get-tuple-element.28), channel_id=1, source_target_pairs={{1,0},{6,4},{9,8},{14,12},{17,16},{22,20},{25,24},{30,28}} | collective-permute-start | bytes 1572872 | tf_op jit(solution)/shard_map/ppermute | solution.py:443
  53.0 40.4 %collective-permute-start.6 = (f32[256,512]{1,0:T(8,128)S(1)}, f32[256,512]{1,0:T(8,128)S(1)}, u32[]{:S(2)}, u32[]{:S(2)}) collective-permute-start(f32[256,512]{1,0:T(8,128)S(1)} %get-tuple-element.21), channel_id=1, source_target_pairs={{1,0},{6,4},{9,8},{14,12},{17,16},{22,20},{25,24},{30,28}} | collective-permute-start | bytes 1572872 | tf_op jit(solution)/shard_map/ppermute | solution.py:443
  54.3 0.7 collective-permute-start.14
  55.0 0.7 collective-permute-start.13
